TPU v7x, 256 devices: a whole 4x4x8 slice. The times are simulated.
256 devices in a mesh: gx: 4 (over x), gy: 64 (over y, z, core).
Axes of the slice: x: 4, y: 4, z: 8, core: 2. Of those that a mesh axis runs over, the one named last changes fastest.
Arguments:
- tile_flux: bfloat16 [4, 12, 8, 1048576], P(None, None, None, ('gx', 'gy')), may hold values from -6 to 6
- tile_frac: float32 [8, 1048576], P(None, ('gx', 'gy')), may hold values from 0.02 to 1
- weights: bfloat16 [256, 7, 16, 256, 128], P(('gx', 'gy')), may hold values from -0.049804688 to 0.14941406
- block_row: int32 [256, 7, 16], P(('gx', 'gy')), may hold values from 0 to 47
- block_col: int32 [256, 7, 16], P(('gx', 'gy')), may hold values from 0 to 31
- send_counts: int32 [256, 7], P(('gx', 'gy')), may hold values from 1 to 16, as said below
Outputs:
- atm_flux: float32 [4, 12, 3145728], P(None, None, ('gx', 'gy'))
Inputs may be any that keep to these rules, and one draw needn't show every extreme that they name: `send_counts`: live slots of a device at an offset; some device has all 7 offsets at 16, and some device receives 16 live slots from every offset.
All inputs are finite; a program needn't handle non-finite values.
Results may differ from a plain program's by a relative error of at most 0.0029.
Values sent between devices are 32-bit elements; how exact they have to be, the bound alone decides.
A program may use at most 128 MiB of HBM per device.

v0:
```python
import jax
import jax.numpy as jnp
from jax import lax
from jax.sharding import PartitionSpec as P

AB_DEV = 48


def shifted(value, axis, steps):
    count = lax.axis_size(axis)
    pairs = [(source, (source + steps) % count) for source in range(count)]
    return lax.ppermute(value, axis, pairs)


def settle(partial_value, targets, blocks_here):
    onehot = (targets[:, None] == jnp.arange(blocks_here, dtype=jnp.float32)[None, :]).astype(
        jnp.float32
    )
    return jnp.einsum("kj,kfr->jfr", onehot, partial_value, precision=lax.Precision.HIGHEST)


def on_device(tile_flux, tile_frac, weights, block_row, block_col, send_counts):
    num_steps = tile_flux.shape[0]
    num_kinds = tile_flux.shape[1]
    num_flux = num_steps * num_kinds
    num_off = weights.shape[1]
    slots = weights.shape[2]
    block_rows = weights.shape[3]
    block_cols = weights.shape[4]
    reach_side = num_off // 2
    frac_sum = jnp.sum(tile_frac, axis=0)
    merged = (
        jnp.sum(tile_flux.astype(jnp.float32) * tile_frac[None, None], axis=2) / frac_sum
    ).astype(jnp.bfloat16)
    land_blocks = merged.reshape(num_flux, -1, block_cols)
    picked = jnp.take(land_blocks, block_col[0].reshape(-1), axis=1)
    picked = picked.reshape(num_flux, num_off, slots, block_cols)
    partial_value = jnp.einsum(
        "okrc,fokc->okfr", weights[0], picked, preferred_element_type=jnp.float32
    )
    active = (jnp.arange(slots, dtype=jnp.int32)[None, :] < send_counts[0][:, None]).astype(
        jnp.float32
    )
    partial_value = partial_value * active[:, :, None, None]
    targets = block_row[0].astype(jnp.float32)
    totals = settle(partial_value[reach_side], targets[reach_side], AB_DEV)
    for offset in range(num_off):
        if offset != reach_side:
            arrived, arrived_rows = shifted(
                (partial_value[offset], targets[offset]), ("gx", "gy"), offset - reach_side
            )
            totals = totals + settle(arrived, arrived_rows, AB_DEV)
    return totals.transpose(1, 0, 2).reshape(num_steps, num_kinds, AB_DEV * block_rows)


def solution(mesh):
    return jax.shard_map(
        on_device,
        mesh=mesh,
        in_specs=(
            P(None, None, None, ("gx", "gy")),
            P(None, ("gx", "gy")),
            P(("gx", "gy"), None, None, None, None),
            P(("gx", "gy"), None, None),
            P(("gx", "gy"), None, None),
            P(("gx", "gy"), None),
        ),
        out_specs=P(None, None, ("gx", "gy")),
        check_vma=False,
    )
```

profile of v0, /device:TPU:1, one launch (start us, length us, event | category | flops | bytes accessed | tf_op | source)
XLA Modules:
  0.0 143.6 jit_solution(351172867749429107)
XLA Ops:
  0.0 0.7 reduce
  0.8 0.8 fusion.45
  1.6 0.9 reduce_sum.22
  2.5 4.0 %multiply_reduce_fusion = f32[4,12,4096]{2,1,0:T(8,128)S(1)} fusion(bf16[4,12,8,4096]{3,2,1,0:T(8,128)(2,1)} %param.6, f32[8,4096]{1,0:T(8,128)} %param.7), kind=kLoop, calls=%fused_computation.3 | loop fusion | flops 4521984 | bytes 4063232 | tf_op jit(solution)/shard_map/reduce_sum | solution.py:33
  6.5 0.2 reduce_sum.21
  6.7 0.5 fusion.22
  7.2 0.8 gather_fusion
  8.0 5.8 %broadcast_multiply_fusion = f32[7,16,48,256]{3,2,1,0:T(8,128)S(1)} fusion(f32[7,16]{1,0:T(8,128)S(1)} %get-tuple-element.19, bf16[1,7,16,256,128]{4,3,2,1,0:T(8,128)(2,1)} %param.8, bf16[48,7,16,128]{3,0,2,1:T(8,128)(2,1)S(1)} %bitcast.67, pred[7,16]{1,0:T(8,128)(4,1)S(1)} %get-tuple-element.20), kind=kOutput, calls=%fused_computation.4 | convolution fusion | flops 354385920 | bytes 14221872 | tf_op jit(solution)/shard_map/okrc,fokc->okfr/dot_general | solution.py:38
  13.8 0.4 slice_bitcast_fusion
  14.2 11.7 %collective-permute-start.1 = (f32[16,48,256]{2,1,0:T(8,128)S(1)}, f32[16,48,256]{2,1,0:T(8,128)S(1)}, u32[]{:S(2)}, u32[]{:S(2)}) collective-permute-start(f32[16,48,256]{2,1,0:T(8,128)S(1)} %get-tuple-element.10), channel_id=1, source_target_pairs={{0,253},{1,254},{2,255},{3,0},{4,1},{5,2},{6,3},{7,4},{8,5},{9,6},... | collective-permute-start | bytes 2359304 | tf_op jit(solution)/shard_map/ppermute | solution.py:12
  25.9 0.7 collective-permute-start.3
  26.7 1.7 %collective-permute-start.10 = (f32[16]{0:T(128)S(1)}, f32[16]{0:T(128)S(1)}, u32[]{:S(2)}, u32[]{:S(2)}) collective-permute-start(f32[16]{0:T(128)S(1)} %get-tuple-element.12), channel_id=1, source_target_pairs={{0,3},{1,4},{2,5},{3,6},{4,7},{5,8},{6,9},{7,10},{8,11},{9,12},{10... | collective-permute-start | bytes 200 | tf_op jit(solution)/shard_map/ppermute | solution.py:12
  28.4 5.5 %collective-permute-start = (f32[16]{0:T(128)S(1)}, f32[16]{0:T(128)S(1)}, u32[]{:S(2)}, u32[]{:S(2)}) collective-permute-start(f32[16]{0:T(128)S(1)} %get-tuple-element.17), channel_id=1, source_target_pairs={{0,253},{1,254},{2,255},{3,0},{4,1},{5,2},{6,3},{7,4},{8,5},{9,6},... | collective-permute-start | bytes 200 | tf_op jit(solution)/shard_map/ppermute | solution.py:12
  33.9 1.5 %collective-permute-start.5 = (f32[16,48,256]{2,1,0:T(8,128)S(1)}, f32[16,48,256]{2,1,0:T(8,128)S(1)}, u32[]{:S(2)}, u32[]{:S(2)}) collective-permute-start(f32[16,48,256]{2,1,0:T(8,128)S(1)} %get-tuple-element.8), channel_id=1, source_target_pairs={{0,255},{1,0},{2,1},{3,2},{4,3},{5,4},{6,5},{7,6},{8,7},{9,8},{10,... | collective-permute-start | bytes 2359304 | tf_op jit(solution)/shard_map/ppermute | solution.py:12
  35.4 1.4 fusion.20
  36.8 31.4 %collective-permute-done = f32[16]{0:T(128)S(1)} collective-permute-done((f32[16]{0:T(128)S(1)}, f32[16]{0:T(128)S(1)}, u32[]{:S(2)}, u32[]{:S(2)}) %collective-permute-start) | collective-permute-done | bytes 96 | tf_op jit(solution)/shard_map/ppermute | solution.py:12
  68.1 0.7 collective-permute-start.2
  68.9 1.8 %collective-permute-start.7 = (f32[16,48,256]{2,1,0:T(8,128)S(1)}, f32[16,48,256]{2,1,0:T(8,128)S(1)}, u32[]{:S(2)}, u32[]{:S(2)}) collective-permute-start(f32[16,48,256]{2,1,0:T(8,128)S(1)} %get-tuple-element.7), channel_id=1, source_target_pairs={{0,1},{1,2},{2,3},{3,4},{4,5},{5,6},{6,7},{7,8},{8,9},{9,10},{10,1... | collective-permute-start | bytes 2359304 | tf_op jit(solution)/shard_map/ppermute | solution.py:12
  70.6 1.4 fusion.18
  72.1 5.9 %collective-permute-start.4 = (f32[16]{0:T(128)S(1)}, f32[16]{0:T(128)S(1)}, u32[]{:S(2)}, u32[]{:S(2)}) collective-permute-start(f32[16]{0:T(128)S(1)} %get-tuple-element.15), channel_id=1, source_target_pairs={{0,255},{1,0},{2,1},{3,2},{4,3},{5,4},{6,5},{7,6},{8,7},{9,8},{10,... | collective-permute-start | bytes 200 | tf_op jit(solution)/shard_map/ppermute | solution.py:12
  78.0 1.4 fusion.16
  79.4 0.1 collective-permute-start.6
  79.5 0.1 collective-permute-start.11
  79.6 1.4 fusion.14
  81.0 9.2 %collective-permute-done.6 = f32[16]{0:T(128)S(1)} collective-permute-done((f32[16]{0:T(128)S(1)}, f32[16]{0:T(128)S(1)}, u32[]{:S(2)}, u32[]{:S(2)}) %collective-permute-start.6) | collective-permute-done | bytes 96 | tf_op jit(solution)/shard_map/ppermute | solution.py:12
  90.2 15.7 %collective-permute-start.8 = (f32[16]{0:T(128)S(1)}, f32[16]{0:T(128)S(1)}, u32[]{:S(2)}, u32[]{:S(2)}) collective-permute-start(f32[16]{0:T(128)S(1)} %get-tuple-element.13), channel_id=1, source_target_pairs={{0,2},{1,3},{2,4},{3,5},{4,6},{5,7},{6,8},{7,9},{8,10},{9,11},{10,... | collective-permute-start | bytes 200 | tf_op jit(solution)/shard_map/ppermute | solution.py:12
  106.0 1.4 fusion.12
  107.4 26.5 %collective-permute-done.8 = f32[16]{0:T(128)S(1)} collective-permute-done((f32[16]{0:T(128)S(1)}, f32[16]{0:T(128)S(1)}, u32[]{:S(2)}, u32[]{:S(2)}) %collective-permute-start.8) | collective-permute-done | bytes 96 | tf_op jit(solution)/shard_map/ppermute | solution.py:12
  133.9 1.4 fusion.10
  135.3 3.4 %add_bitcast_fusion = f32[48,48,256]{2,1,0:T(8,128)} fusion(f32[48,48,256]{2,0,1:T(8,128)S(1)} %fusion.10, f32[48,48,256]{2,0,1:T(8,128)S(1)} %fusion.12, f32[48,48,256]{2,0,1:T(8,128)S(1)} %fusion.14, f32[48,48,256]{2,0,1:T(8,128)S(1)} %fusion.16, f32[48,48,256]{2,0,1:T(8,128)S(1)} %fusion.20, f32[48,48,256]{2,0,1:T(8,128)S(1)} %fusion.18, ...), kind=kOutput, calls=%fused_computation.5 | convolution fusion | flops 116785920 | bytes 17301568 | tf_op jit(solution)/shard_map/kj,kfr->jfr/dot_general | solution.py:19
  138.7 1.9 %reshape.94 = f32[4,12,12288]{2,1,0:T(8,128)S(1)} reshape(f32[48,48,256]{2,1,0:T(8,128)} %add_bitcast_fusion) | data formatting | bytes 4718592 | tf_op jit(solution)/shard_map/reshape | solution.py:53
  140.7 2.9 %copy.23 = f32[4,12,12288]{2,0,1:T(4,128)} copy(f32[4,12,12288]{2,1,0:T(8,128)S(1)} %reshape.94) | data formatting | bytes 4718592 | tf_op jit(solution)/shard_map/reshape | solution.py:53
  (17 shorter events, 0.1 us)
Async XLA Ops:
  13.8 12.8 %copy-start = (s32[1,7,16]{2,0,1:T(1,128)S(1)}, s32[1,7,16]{2,0,1:T(1,128)}, u32[]{:S(2)}) copy-start(s32[1,7,16]{2,0,1:T(1,128)} %param.9) | copy-start | bytes 1348
  14.2 54.6 %collective-permute-start.1 = (f32[16,48,256]{2,1,0:T(8,128)S(1)}, f32[16,48,256]{2,1,0:T(8,128)S(1)}, u32[]{:S(2)}, u32[]{:S(2)}) collective-permute-start(f32[16,48,256]{2,1,0:T(8,128)S(1)} %get-tuple-element.10), channel_id=1, source_target_pairs={{0,253},{1,254},{2,255},{3,0},{4,1},{5,2},{6,3},{7,4},{8,5},{9,6},... | collective-permute-start | bytes 2359304 | tf_op jit(solution)/shard_map/ppermute | solution.py:12
  25.9 52.0 %collective-permute-start.3 = (f32[16,48,256]{2,1,0:T(8,128)S(1)}, f32[16,48,256]{2,1,0:T(8,128)S(1)}, u32[]{:S(2)}, u32[]{:S(2)}) collective-permute-start(f32[16,48,256]{2,1,0:T(8,128)S(1)} %get-tuple-element.9), channel_id=1, source_target_pairs={{0,254},{1,255},{2,0},{3,1},{4,2},{5,3},{6,4},{7,5},{8,6},{9,7},{1... | collective-permute-start | bytes 2359304 | tf_op jit(solution)/shard_map/ppermute | solution.py:12
  26.7 108.7 %collective-permute-start.10 = (f32[16]{0:T(128)S(1)}, f32[16]{0:T(128)S(1)}, u32[]{:S(2)}, u32[]{:S(2)}) collective-permute-start(f32[16]{0:T(128)S(1)} %get-tuple-element.12), channel_id=1, source_target_pairs={{0,3},{1,4},{2,5},{3,6},{4,7},{5,8},{6,9},{7,10},{8,11},{9,12},{10... | collective-permute-start | bytes 200 | tf_op jit(solution)/shard_map/ppermute | solution.py:12
  28.4 39.8 %collective-permute-start = (f32[16]{0:T(128)S(1)}, f32[16]{0:T(128)S(1)}, u32[]{:S(2)}, u32[]{:S(2)}) collective-permute-start(f32[16]{0:T(128)S(1)} %get-tuple-element.17), channel_id=1, source_target_pairs={{0,253},{1,254},{2,255},{3,0},{4,1},{5,2},{6,3},{7,4},{8,5},{9,6},... | collective-permute-start | bytes 200 | tf_op jit(solution)/shard_map/ppermute | solution.py:12
  33.9 45.6 %collective-permute-start.5 = (f32[16,48,256]{2,1,0:T(8,128)S(1)}, f32[16,48,256]{2,1,0:T(8,128)S(1)}, u32[]{:S(2)}, u32[]{:S(2)}) collective-permute-start(f32[16,48,256]{2,1,0:T(8,128)S(1)} %get-tuple-element.8), channel_id=1, source_target_pairs={{0,255},{1,0},{2,1},{3,2},{4,3},{5,4},{6,5},{7,6},{8,7},{9,8},{10,... | collective-permute-start | bytes 2359304 | tf_op jit(solution)/shard_map/ppermute | solution.py:12
  68.1 3.9 %collective-permute-start.2 = (f32[16]{0:T(128)S(1)}, f32[16]{0:T(128)S(1)}, u32[]{:S(2)}, u32[]{:S(2)}) collective-permute-start(f32[16]{0:T(128)S(1)} %get-tuple-element.16), channel_id=1, source_target_pairs={{0,254},{1,255},{2,0},{3,1},{4,2},{5,3},{6,4},{7,5},{8,6},{9,7},{1... | collective-permute-start | bytes 200 | tf_op jit(solution)/shard_map/ppermute | solution.py:12
  68.9 37.1 %collective-permute-start.7 = (f32[16,48,256]{2,1,0:T(8,128)S(1)}, f32[16,48,256]{2,1,0:T(8,128)S(1)}, u32[]{:S(2)}, u32[]{:S(2)}) collective-permute-start(f32[16,48,256]{2,1,0:T(8,128)S(1)} %get-tuple-element.7), channel_id=1, source_target_pairs={{0,1},{1,2},{2,3},{3,4},{4,5},{5,6},{6,7},{7,8},{8,9},{9,10},{10,1... | collective-permute-start | bytes 2359304 | tf_op jit(solution)/shard_map/ppermute | solution.py:12
  72.1 7.3 %collective-permute-start.4 = (f32[16]{0:T(128)S(1)}, f32[16]{0:T(128)S(1)}, u32[]{:S(2)}, u32[]{:S(2)}) collective-permute-start(f32[16]{0:T(128)S(1)} %get-tuple-element.15), channel_id=1, source_target_pairs={{0,255},{1,0},{2,1},{3,2},{4,3},{5,4},{6,5},{7,6},{8,7},{9,8},{10,... | collective-permute-start | bytes 200 | tf_op jit(solution)/shard_map/ppermute | solution.py:12
  78.0 55.9 %collective-permute-start.9 = (f32[16,48,256]{2,1,0:T(8,128)S(1)}, f32[16,48,256]{2,1,0:T(8,128)S(1)}, u32[]{:S(2)}, u32[]{:S(2)}) collective-permute-start(f32[16,48,256]{2,1,0:T(8,128)S(1)} %get-tuple-element.6), channel_id=1, source_target_pairs={{0,2},{1,3},{2,4},{3,5},{4,6},{5,7},{6,8},{7,9},{8,10},{9,11},{10,... | collective-permute-start | bytes 2359304 | tf_op jit(solution)/shard_map/ppermute | solution.py:12
  79.4 10.8 %collective-permute-start.6 = (f32[16]{0:T(128)S(1)}, f32[16]{0:T(128)S(1)}, u32[]{:S(2)}, u32[]{:S(2)}) collective-permute-start(f32[16]{0:T(128)S(1)} %get-tuple-element.14), channel_id=1, source_target_pairs={{0,1},{1,2},{2,3},{3,4},{4,5},{5,6},{6,7},{7,8},{8,9},{9,10},{10,1... | collective-permute-start | bytes 200 | tf_op jit(solution)/shard_map/ppermute | solution.py:12
  79.5 55.8 %collective-permute-start.11 = (f32[16,48,256]{2,1,0:T(8,128)S(1)}, f32[16,48,256]{2,1,0:T(8,128)S(1)}, u32[]{:S(2)}, u32[]{:S(2)}) collective-permute-start(f32[16,48,256]{2,1,0:T(8,128)S(1)} %get-tuple-element.5), channel_id=1, source_target_pairs={{0,3},{1,4},{2,5},{3,6},{4,7},{5,8},{6,9},{7,10},{8,11},{9,12},{10... | collective-permute-start | bytes 2359304 | tf_op jit(solution)/shard_map/ppermute | solution.py:12
  90.2 43.7 %collective-permute-start.8 = (f32[16]{0:T(128)S(1)}, f32[16]{0:T(128)S(1)}, u32[]{:S(2)}, u32[]{:S(2)}) collective-permute-start(f32[16]{0:T(128)S(1)} %get-tuple-element.13), channel_id=1, source_target_pairs={{0,2},{1,3},{2,4},{3,5},{4,6},{5,7},{6,8},{7,9},{8,10},{9,11},{10,... | collective-permute-start | bytes 200 | tf_op jit(solution)/shard_map/ppermute | solution.py:12
where the time goes:
time: 144 us
  waiting for transfers between devices  67 us (47%)
  starting transfers between devices  45.4 us (32%)
  matrix products  17.8 us (12%)
  other arithmetic  6.87 us (5%)
  local copies, waits for them, and re-layouts  6.33 us (4%)
    ppermute x12, waiting for transfers between devices, shifted(): return lax.ppermute(value, axis, pairs)  67 us
    ppermute x12, starting transfers between devices, shifted(): return lax.ppermute(value, axis, pairs)  45.4 us
    dot_general x7, matrix products, settle(): jnp.einsum('kj,kfr->jfr', onehot, partial_value, precision=lax.Precision....  12 us
    dot_general x1, matrix products, on_device(): jnp.einsum('okrc,fokc->okfr', weights[0], picked, preferred_element_type=...  5.81 us
    reshape x2, local copies, waits for them, and re-layouts, on_device(): totals.transpose(1, 0, 2).reshape(num_steps, num_kinds, AB_DEV * block_rows)  4.82 us
    reduce_sum x1, other arithmetic, on_device(): jnp.sum(tile_flux.astype(jnp.float32) * tile_frac[None, None], axis=2)  3.97 us
  transfers between devices with their start and end apart: 12, of which 3 were waited for; matrix products, arithmetic and copies ran while one was open for 6% of the time, Pallas kernels for 0%

commit v1 on v0

v1 whole, which is shorter than its diff:
```python
import functools

import jax
import jax.numpy as jnp
from jax import lax
from jax.experimental import pallas as pl
from jax.experimental.pallas import tpu as pltpu
from jax.sharding import PartitionSpec as P

MESH = pl.DeviceIdType.MESH
AB_DEV = 48
CHUNK = 4
FLUX_CHUNKS = 4


def combine(a, b, shift, mask):
    return jnp.where(mask, a + pltpu.roll(a, 8 - shift, 0), b + pltpu.roll(b, shift, 0))


def sum_rows(parts):
    row = lax.broadcasted_iota(jnp.int32, (8, 128), 0)
    top = [combine(parts[r], parts[r + 4], 4, row < 4) for r in range(4)]
    mid = [combine(top[r], top[r + 2], 2, (row & 2) == 0) for r in range(2)]
    return combine(mid[0], mid[1], 1, (row & 1) == 0)


def send_kernel(
    sizes,
    flux_hbm, frac_hbm, weights_hbm, rows_hbm, col_ref, count_ref,
    arrived_hbm, tables_hbm,
    flux_ref, frac_ref, weights_ref, merged_ref, staged_ref,
    in_sem, weight_sem, own_sem, send_sem, recv_sem, table_send, table_recv,
):
    num_x, num_y = sizes
    devices = num_x * num_y
    num_step, num_kind = flux_ref.shape[:2]
    num_off, slots = weights_ref.shape[:2]
    reach = num_off // 2
    land_blocks = merged_ref.shape[0]
    chunks = slots // CHUNK
    sends = chunks * (num_off - 1)
    wide = flux_ref.shape[3] // FLUX_CHUNKS
    me = lax.axis_index("gx") * num_y + lax.axis_index("gy")

    def flux_copy(part):
        cells = pl.ds(part * wide, wide)
        return pltpu.make_async_copy(
            flux_hbm.at[:, :, :, cells], flux_ref.at[:, :, :, cells], in_sem.at[part]
        )

    def plan(i):
        chunk = i // (num_off - 1)
        turn = i % (num_off - 1)
        off = (reach - turn // 2) * (1 - 2 * (turn % 2))
        return chunk, off

    def weight_copy(chunk, offset, sem):
        part = (offset, pl.ds(chunk * CHUNK, CHUNK))
        return pltpu.make_async_copy(weights_hbm.at[part], weights_ref.at[part], sem)

    def target(off):
        there = (me + off + devices) % devices
        return (there // num_y, there % num_y)

    frac_copy = pltpu.make_async_copy(frac_hbm, frac_ref, in_sem.at[FLUX_CHUNKS])
    frac_copy.start()
    for part in range(FLUX_CHUNKS):
        flux_copy(part).start()

    @pl.loop(0, sends)
    def _(i):
        chunk, off = plan(i)
        weight_copy(chunk, off + reach, weight_sem.at[i]).start()

    @pl.loop(0, chunks)
    def _(chunk):
        weight_copy(chunk, reach, weight_sem.at[sends + chunk]).start()

    barrier = pltpu.get_barrier_semaphore()
    for off in range(-reach, reach + 1):
        if off:
            pl.semaphore_signal(barrier, inc=1, device_id=target(off), device_id_type=MESH)

    frac_copy.wait()

    def merge_block(block):
        cells = pl.ds(pl.multiple_of(block * 128, 128), 128)
        frac = frac_ref[:, cells]
        total = jnp.sum(frac, axis=0, keepdims=True)
        pieces = []
        for first in range(0, num_step * num_kind, 8):
            parts = []
            for line in range(first, first + 8):
                kind, step = line // num_step, line % num_step
                parts.append(flux_ref[step, kind, :, cells].astype(jnp.float32) * frac)
            pieces.append(sum_rows(parts) / total)
        merged_ref[block] = jnp.concatenate(pieces, axis=0).astype(jnp.bfloat16)

    per_part = land_blocks // FLUX_CHUNKS
    for part in range(FLUX_CHUNKS):
        flux_copy(part).wait()
        pl.loop(part * per_part, (part + 1) * per_part)(merge_block)

    pl.semaphore_wait(barrier, num_off - 1)

    def table_copy(off):
        return pltpu.make_async_remote_copy(
            src_ref=rows_hbm,
            dst_ref=tables_hbm.at[off + reach],
            send_sem=table_send.at[off + reach],
            recv_sem=table_recv.at[off + reach],
            device_id=target(off),
            device_id_type=MESH,
        )

    def partial_sums(chunk, offset):
        for step in range(CHUNK):
            slot = chunk * CHUNK + step
            picked = merged_ref[col_ref[offset, slot]]
            picked = jnp.where(slot < count_ref[offset], picked, jnp.zeros_like(picked))
            staged_ref[offset, slot] = lax.dot_general(
                picked, weights_ref[offset, slot], (((1,), (1,)), ((), ())),
                preferred_element_type=jnp.float32,
            )

    def chunk_copy(i):
        chunk, off = plan(i)
        part = (off + reach, pl.ds(chunk * CHUNK, CHUNK))
        return pltpu.make_async_remote_copy(
            src_ref=staged_ref.at[part],
            dst_ref=arrived_hbm.at[part],
            send_sem=send_sem.at[i],
            recv_sem=recv_sem.at[i],
            device_id=target(off),
            device_id_type=MESH,
        )

    @pl.loop(0, sends)
    def _(i):
        chunk, off = plan(i)
        weight_copy(chunk, off + reach, weight_sem.at[i]).wait()
        partial_sums(chunk, off + reach)

        @pl.when(i > 0)
        def _():
            chunk_copy(i - 1).start()

    for off in range(-reach, reach + 1):
        if off:
            table_copy(off).start()
    chunk_copy(sends - 1).start()

    @pl.loop(0, chunks)
    def _(chunk):
        weight_copy(chunk, reach, weight_sem.at[sends + chunk]).wait()
        partial_sums(chunk, reach)

    own = pltpu.make_async_copy(staged_ref.at[reach], arrived_hbm.at[reach], own_sem)
    own.start()
    own_table = pltpu.make_async_copy(rows_hbm, tables_hbm.at[reach], in_sem.at[0])
    own_table.start()

    @pl.loop(0, sends)
    def _(i):
        chunk_copy(i).wait()

    for off in range(-reach, reach + 1):
        if off:
            table_copy(off).wait()
    own.wait()
    own_table.wait()


def settle_kernel(table_ref, arrived_hbm, out_hbm, arrived_ref, total_ref, out_ref, in_sem, out_sem):
    num_off, slots, lines, block_rows = arrived_ref.shape
    num_kind, num_step = out_ref.shape[:2]
    atm_blocks = total_ref.shape[0]
    parts = 4

    def fetch(offset):
        return pltpu.make_async_copy(arrived_hbm.at[offset], arrived_ref.at[offset], in_sem.at[offset])

    for offset in range(num_off):
        fetch(offset).start()

    @pl.loop(0, atm_blocks)
    def _(block):
        total_ref[block] = jnp.zeros((lines, block_rows), jnp.float32)

    for offset in range(num_off):
        fetch(offset).wait()

        @pl.loop(0, slots)
        def _(slot, offset=offset):
            block = table_ref[offset, offset, slot]
            total_ref[block] = total_ref[block] + arrived_ref[offset, slot]

    per_part = atm_blocks // parts

    def emit(part):
        cells = pl.ds(part * per_part * block_rows, per_part * block_rows)
        return pltpu.make_async_copy(out_ref.at[:, :, cells], out_hbm.at[:, :, cells], out_sem.at[part])

    for part in range(parts):

        @pl.loop(part * per_part, (part + 1) * per_part)
        def _(block):
            cells = pl.ds(pl.multiple_of(block * block_rows, block_rows), block_rows)
            for kind in range(num_kind):
                out_ref[kind, :, cells] = total_ref[block, pl.ds(kind * num_step, num_step), :]

        emit(part).start()
    for part in range(parts):
        emit(part).wait()


def on_device(sizes, tile_flux, tile_frac, weights, block_row, block_col, send_counts):
    num_step, num_kind, _, cells = tile_flux.shape
    num_off, slots, block_rows, block_cols = weights.shape[1:]
    lines = num_step * num_kind
    sends = slots // CHUNK * (num_off - 1)
    arrived, tables = pl.pallas_call(
        functools.partial(send_kernel, sizes),
        out_shape=(
            jax.ShapeDtypeStruct((num_off, slots, lines, block_rows), jnp.float32),
            jax.ShapeDtypeStruct((num_off, num_off, slots), jnp.int32),
        ),
        in_specs=[pl.BlockSpec(memory_space=pl.ANY)] * 4
        + [pl.BlockSpec(memory_space=pltpu.SMEM)] * 2,
        out_specs=(pl.BlockSpec(memory_space=pl.ANY), pl.BlockSpec(memory_space=pl.ANY)),
        scratch_shapes=[
            pltpu.VMEM(tile_flux.shape, jnp.bfloat16),
            pltpu.VMEM(tile_frac.shape, jnp.float32),
            pltpu.VMEM(weights.shape[1:], jnp.bfloat16),
            pltpu.VMEM((cells // block_cols, lines, block_cols), jnp.bfloat16),
            pltpu.VMEM((num_off, slots, lines, block_rows), jnp.float32),
            pltpu.SemaphoreType.DMA((FLUX_CHUNKS + 1,)),
            pltpu.SemaphoreType.DMA((slots // CHUNK * num_off,)),
            pltpu.SemaphoreType.DMA,
            pltpu.SemaphoreType.DMA((sends,)),
            pltpu.SemaphoreType.DMA((sends,)),
            pltpu.SemaphoreType.DMA((num_off,)),
            pltpu.SemaphoreType.DMA((num_off,)),
        ],
        compiler_params=pltpu.CompilerParams(
            collective_id=0, has_side_effects=True, vmem_limit_bytes=40 * 1024 * 1024
        ),
    )(tile_flux, tile_frac, weights[0], block_row[0], block_col[0], send_counts[0])
    settled = pl.pallas_call(
        settle_kernel,
        out_shape=jax.ShapeDtypeStruct((num_kind, num_step, AB_DEV * block_rows), jnp.float32),
        in_specs=[pl.BlockSpec(memory_space=pltpu.SMEM), pl.BlockSpec(memory_space=pl.ANY)],
        out_specs=pl.BlockSpec(memory_space=pl.ANY),
        scratch_shapes=[
            pltpu.VMEM((num_off, slots, lines, block_rows), jnp.float32),
            pltpu.VMEM((AB_DEV, lines, block_rows), jnp.float32),
            pltpu.VMEM((num_kind, num_step, AB_DEV * block_rows), jnp.float32),
            pltpu.SemaphoreType.DMA((num_off,)),
            pltpu.SemaphoreType.DMA((4,)),
        ],
        compiler_params=pltpu.CompilerParams(vmem_limit_bytes=24 * 1024 * 1024),
    )(tables, arrived)
    return settled.transpose(1, 0, 2)


def solution(mesh):
    sizes = (mesh.shape["gx"], mesh.shape["gy"])
    return jax.shard_map(
        functools.partial(on_device, sizes),
        mesh=mesh,
        in_specs=(
            P(None, None, None, ("gx", "gy")),
            P(None, ("gx", "gy")),
            P(("gx", "gy"), None, None, None, None),
            P(("gx", "gy"), None, None),
            P(("gx", "gy"), None, None),
            P(("gx", "gy"), None),
        ),
        out_specs=P(None, None, ("gx", "gy")),
        check_vma=False,
    )
```

time: 144 us -> 76.6 us (0.53)
  Pallas kernels: 0 us -> 72.3 us
  waiting for transfers between devices: 67 us -> 0 us
  starting transfers between devices: 45.4 us -> 0 us
  matrix products: 17.8 us -> 0 us
  other arithmetic: 6.87 us -> 0 us
  local copies, waits for them, and re-layouts: 6.33 us -> 4.15 us
    pallas_call x0 -> x2, Pallas kernels: none -> 72.3 us  [the longest x1 67.8 us: on_device(): pl.pallas_call(functools.partial(send_kernel, sizes), out_shape=(jax.Shap...]
    ppermute x12 -> x0, waiting for transfers between devices: 67 us -> none  [shifted(): return lax.ppermute(value, axis, pairs)]
    ppermute x12 -> x0, starting transfers between devices: 45.4 us -> none  [shifted(): return lax.ppermute(value, axis, pairs)]
    dot_general x8 -> x0, matrix products: 17.8 us -> none  [the longest x7 12 us: settle(): jnp.einsum('kj,kfr->jfr', onehot, partial_value, precision=lax.Precision....]
    reduce_sum x2 -> x0, other arithmetic: 4.9 us -> none  [the longest x1 3.97 us: on_device(): jnp.sum(tile_flux.astype(jnp.float32) * tile_frac[None, None], axis=2)]
    reshape x2 -> x0, local copies, waits for them, and re-layouts: 4.82 us -> none  [on_device(): totals.transpose(1, 0, 2).reshape(num_steps, num_kinds, AB_DEV * block_rows)]
    unnamed x2 -> x7, local copies, waits for them, and re-layouts: 0.01 us -> 4.15 us
  transfers between devices with their start and end apart: 12 -> 0, of which waited for: 3 -> 0; matrix products, arithmetic and copies ran while one was open for 6% -> 0% of each run, Pallas kernels for 0% -> 0%
where the time goes in v1:
time: 76.6 us; the launch traced here: 76.5 us
  Pallas kernels  72.3 us (94%)
  local copies, waits for them, and re-layouts  4.15 us (5%)
    pallas_call x1, Pallas kernels, on_device(): pl.pallas_call(functools.partial(send_kernel, sizes), out_shape=(jax.Shap...  67.8 us
    pallas_call x1, Pallas kernels, on_device(): pl.pallas_call(settle_kernel, out_shape=jax.ShapeDtypeStruct((num_kind, n...  4.55 us
    unnamed x7, local copies, waits for them, and re-layouts  4.15 us

profile of v1, /device:TPU:1, one launch (start us, length us, event | category | flops | bytes accessed | tf_op | source)
XLA Modules:
  0.0 76.5 jit_solution(17177181289967510321)
XLA Ops:
  0.0 0.7 copy_bitcast_fusion
  0.7 0.0 copy-start
  0.7 1.9 %copy-done = bf16[4,12,8,4096]{3,2,1,0:T(8,128)(2,1)S(1)} copy-done((bf16[4,12,8,4096]{3,2,1,0:T(8,128)(2,1)S(1)}, bf16[4,12,8,4096]{3,2,1,0:T(8,128)(2,1)}, u32[]{:S(2)}) %copy-start) | copy-done | bytes 3145752
  2.6 0.0 copy-start.1
  2.6 0.9 %copy-done.1 = f32[8,4096]{1,0:T(8,128)S(1)} copy-done((f32[8,4096]{1,0:T(8,128)S(1)}, f32[8,4096]{1,0:T(8,128)}, u32[]{:S(2)}) %copy-start.1) | copy-done | bytes 131096
  3.5 0.0 copy-start.2
  3.5 0.7 copy-done.2
  4.2 67.8 %shard_map.64 = (f32[7,16,48,256]{3,2,1,0:T(8,128)S(1)}, s32[7,7,16]{2,1,0:T(8,128)S(1)}) custom-call(bf16[4,12,8,4096]{3,2,1,0:T(8,128)(2,1)S(1)} %copy-done, f32[8,4096]{1,0:T(8,128)S(1)} %copy-done.1, bf16[7,16,256,128]{3,2,1,0:T(8,128)(2,1)} %bitcast.8, s32[7,16]{1,0:T(8,128)S(1)} %get-tuple-element.10.rows_hbm, s32[7,16]{1,0:T(8,128)S(1)} %get-tuple-element.9.col_ref, ...), custom_call_target="tpu_custom_call" | custom-call | tf_op jit(solution)/shard_map/pallas_call | solution.py:222
  71.9 4.5 %shard_map.65 = f32[12,4,12288]{2,1,0:T(4,128)} custom-call(s32[7,7,16]{2,1,0:T(8,128)S(1)} %get-tuple-element.7.table_ref, f32[7,16,48,256]{3,2,1,0:T(8,128)S(1)} %get-tuple-element.8.arrived_hbm), custom_call_target="tpu_custom_call" | custom-call | tf_op jit(solution)/shard_map/pallas_call | solution.py:249
Async XLA Ops:
  0.7 1.9 %copy-start = (bf16[4,12,8,4096]{3,2,1,0:T(8,128)(2,1)S(1)}, bf16[4,12,8,4096]{3,2,1,0:T(8,128)(2,1)}, u32[]{:S(2)}) copy-start(bf16[4,12,8,4096]{3,2,1,0:T(8,128)(2,1)} %flux_hbm.1) | copy-start | bytes 9437188
  2.6 0.9 %copy-start.1 = (f32[8,4096]{1,0:T(8,128)S(1)}, f32[8,4096]{1,0:T(8,128)}, u32[]{:S(2)}) copy-start(f32[8,4096]{1,0:T(8,128)} %frac_hbm.1) | copy-start | bytes 393220
  3.5 0.7 copy-start.2

commit v2 on v1

v2 whole, which is shorter than its diff:
```python
import functools

import jax
import jax.numpy as jnp
from jax import lax
from jax.experimental import pallas as pl
from jax.experimental.pallas import tpu as pltpu
from jax.sharding import PartitionSpec as P

MESH = pl.DeviceIdType.MESH
AB_DEV = 48
CHUNK = 3
FLUX_CHUNKS = 4


def combine(a, b, shift, mask):
    return jnp.where(mask, a + pltpu.roll(a, 8 - shift, 0), b + pltpu.roll(b, shift, 0))


def sum_rows(parts):
    row = lax.broadcasted_iota(jnp.int32, (8, 128), 0)
    top = [combine(parts[r], parts[r + 4], 4, row < 4) for r in range(4)]
    mid = [combine(top[r], top[r + 2], 2, (row & 2) == 0) for r in range(2)]
    return combine(mid[0], mid[1], 1, (row & 1) == 0)


def send_kernel(
    sizes,
    flux_hbm, frac_hbm, weights_hbm, rows_hbm, col_hbm, count_hbm,
    arrived_hbm, tables_hbm,
    flux_ref, frac_ref, weights_ref, merged_ref, staged_ref, col_ref, count_ref,
    in_sem, first_weight, weight_sem, own_sem, first_send, first_recv, send_sem, recv_sem, table_send, table_recv,
):
    num_x, num_y = sizes
    devices = num_x * num_y
    num_step, num_kind = flux_ref.shape[:2]
    num_off, slots = weights_ref.shape[:2]
    reach = num_off // 2
    others = num_off - 1
    land_blocks = merged_ref.shape[0]
    chunks = (slots - 1) // CHUNK
    sends = chunks * others
    wide = land_blocks // FLUX_CHUNKS
    me = lax.axis_index("gx") * num_y + lax.axis_index("gy")

    def flux_copy(part):
        blocks = pl.ds(part * wide, wide)
        return pltpu.make_async_copy(
            flux_hbm.at[:, :, blocks], flux_ref.at[:, :, blocks], in_sem.at[part]
        )

    def offset_of(turn):
        return (reach - turn // 2) * (1 - 2 * (turn % 2))

    def plan(i):
        return i // others, offset_of(i % others)

    def chunk_part(chunk, offset):
        return offset, pl.ds(1 + chunk * CHUNK, CHUNK)

    def weight_copy(part, sem):
        return pltpu.make_async_copy(weights_hbm.at[part], weights_ref.at[part], sem)

    def first_part(offset):
        return offset, pl.ds(0, 1)

    def target(off):
        there = (me + off + devices) % devices
        return (there // num_y, there % num_y)

    col_copy = pltpu.make_async_copy(col_hbm, col_ref, in_sem.at[FLUX_CHUNKS + 1])
    count_copy = pltpu.make_async_copy(count_hbm, count_ref, in_sem.at[FLUX_CHUNKS + 2])
    frac_copy = pltpu.make_async_copy(frac_hbm, frac_ref, in_sem.at[FLUX_CHUNKS])
    col_copy.start()
    count_copy.start()
    frac_copy.start()
    for part in range(FLUX_CHUNKS):
        flux_copy(part).start()

    barrier = pltpu.get_barrier_semaphore()
    for off in range(-reach, reach + 1):
        if off:
            pl.semaphore_signal(barrier, inc=1, device_id=target(off), device_id_type=MESH)

    for offset in range(num_off):
        weight_copy(first_part(offset), first_weight.at[offset]).start()

    @pl.loop(0, sends)
    def _(i):
        chunk, off = plan(i)
        weight_copy(chunk_part(chunk, off + reach), weight_sem.at[i]).start()

    @pl.loop(0, chunks)
    def _(chunk):
        weight_copy(chunk_part(chunk, reach), weight_sem.at[sends + chunk]).start()

    def merge(block):
        frac = frac_ref[block]
        total = jnp.sum(frac, axis=0, keepdims=True)
        pieces = []
        for first in range(0, num_step * num_kind, 8):
            parts = []
            for line in range(first, first + 8):
                kind, step = line // num_step, line % num_step
                parts.append(flux_ref[step, kind, block].astype(jnp.float32) * frac)
            pieces.append(sum_rows(parts) / total)
        return jnp.concatenate(pieces, axis=0).astype(jnp.bfloat16)

    def table_copy(off):
        return pltpu.make_async_remote_copy(
            src_ref=rows_hbm,
            dst_ref=tables_hbm.at[off + reach],
            send_sem=table_send.at[off + reach],
            recv_sem=table_recv.at[off + reach],
            device_id=target(off),
            device_id_type=MESH,
        )

    def remote(part, off, to_sem, from_sem):
        return pltpu.make_async_remote_copy(
            src_ref=staged_ref.at[part],
            dst_ref=arrived_hbm.at[part],
            send_sem=to_sem,
            recv_sem=from_sem,
            device_id=target(off),
            device_id_type=MESH,
        )

    def first_copy(turn):
        off = offset_of(turn)
        return remote(first_part(off + reach), off, first_send.at[turn], first_recv.at[turn])

    def chunk_copy(i):
        chunk, off = plan(i)
        return remote(chunk_part(chunk, off + reach), off, send_sem.at[i], recv_sem.at[i])

    def multiply(picked, offset, slot):
        picked = jnp.where(slot < count_ref[0, offset], picked, jnp.zeros_like(picked))
        staged_ref[offset, slot] = lax.dot_general(
            picked, weights_ref[offset, slot], (((1,), (1,)), ((), ())),
            preferred_element_type=jnp.float32,
        )

    def multiply_chunk(chunk, offset):
        for step in range(CHUNK):
            slot = 1 + chunk * CHUNK + step
            multiply(merged_ref[col_ref[offset, 0, slot]], offset, slot)

    col_copy.wait()
    count_copy.wait()
    frac_copy.wait()
    for part in range(FLUX_CHUNKS):
        flux_copy(part).wait()
    pl.semaphore_wait(barrier, others)

    @pl.loop(0, others)
    def _(turn):
        offset = offset_of(turn) + reach
        weight_copy(first_part(offset), first_weight.at[offset]).wait()
        multiply(merge(col_ref[offset, 0, 0]), offset, 0)

        @pl.when(turn > 0)
        def _():
            first_copy(turn - 1).start()

    for off in range(-reach, reach + 1):
        if off:
            table_copy(off).start()
    first_copy(others - 1).start()

    @pl.loop(0, land_blocks)
    def _(block):
        merged_ref[block] = merge(block)

    @pl.loop(0, sends)
    def _(i):
        chunk, off = plan(i)
        weight_copy(chunk_part(chunk, off + reach), weight_sem.at[i]).wait()
        multiply_chunk(chunk, off + reach)

        @pl.when(i > 0)
        def _():
            chunk_copy(i - 1).start()

    weight_copy(first_part(reach), first_weight.at[reach]).wait()
    multiply(merged_ref[col_ref[reach, 0, 0]], reach, 0)
    chunk_copy(sends - 1).start()

    @pl.loop(0, chunks)
    def _(chunk):
        weight_copy(chunk_part(chunk, reach), weight_sem.at[sends + chunk]).wait()
        multiply_chunk(chunk, reach)

    own_table = pltpu.make_async_copy(rows_hbm, tables_hbm.at[reach], in_sem.at[0])
    own_table.start()
    own = pltpu.make_async_copy(staged_ref.at[reach], arrived_hbm.at[reach], own_sem)
    own.start()

    @pl.loop(0, others)
    def _(turn):
        first_copy(turn).wait()

    @pl.loop(0, sends)
    def _(i):
        chunk_copy(i).wait()

    for off in range(-reach, reach + 1):
        if off:
            table_copy(off).wait()
    own.wait()
    own_table.wait()


def settle_kernel(table_ref, arrived_ref, out_hbm, total_ref, out_ref, out_sem):
    num_off, slots, lines, block_rows = arrived_ref.shape
    num_kind, num_step = out_ref.shape[:2]
    atm_blocks = total_ref.shape[0]
    parts = 4

    @pl.loop(0, atm_blocks, unroll=4)
    def _(block):
        total_ref[block] = jnp.zeros((lines, block_rows), jnp.float32)

    for offset in range(num_off):

        @pl.loop(0, slots, unroll=4)
        def _(slot, offset=offset):
            block = table_ref[offset, offset, 0, slot]
            total_ref[block] = total_ref[block] + arrived_ref[offset, slot]

    per_part = atm_blocks // parts

    def emit(part):
        cells = pl.ds(part * per_part * block_rows, per_part * block_rows)
        return pltpu.make_async_copy(out_ref.at[:, :, cells], out_hbm.at[:, :, cells], out_sem.at[part])

    for part in range(parts):

        @pl.loop(part * per_part, (part + 1) * per_part, unroll=2)
        def _(block):
            cells = pl.ds(pl.multiple_of(block * block_rows, block_rows), block_rows)
            for kind in range(num_kind):
                out_ref[kind, :, cells] = total_ref[block, pl.ds(kind * num_step, num_step), :]

        emit(part).start()
    for part in range(parts):
        emit(part).wait()


def on_device(sizes, tile_flux, tile_frac, weights, block_row, block_col, send_counts):
    num_step, num_kind, tiles, cells = tile_flux.shape
    num_off, slots, block_rows, block_cols = weights.shape[1:]
    lines = num_step * num_kind
    chunks = (slots - 1) // CHUNK
    sends = chunks * (num_off - 1)
    tile_flux = tile_flux.reshape(num_step, num_kind, tiles, -1, block_cols).transpose(0, 1, 3, 2, 4)
    tile_frac = tile_frac.reshape(tiles, -1, block_cols).transpose(1, 0, 2)
    arrived, tables = pl.pallas_call(
        functools.partial(send_kernel, sizes),
        out_shape=(
            jax.ShapeDtypeStruct((num_off, slots, lines, block_rows), jnp.float32),
            jax.ShapeDtypeStruct((num_off, num_off, 1, slots), jnp.int32),
        ),
        in_specs=[pl.BlockSpec(memory_space=pltpu.HBM)] * 6,
        out_specs=(pl.BlockSpec(memory_space=pl.ANY), pl.BlockSpec(memory_space=pl.ANY)),
        scratch_shapes=[
            pltpu.VMEM(tile_flux.shape, jnp.bfloat16),
            pltpu.VMEM(tile_frac.shape, jnp.float32),
            pltpu.VMEM(weights.shape[1:], jnp.bfloat16),
            pltpu.VMEM((cells // block_cols, lines, block_cols), jnp.bfloat16),
            pltpu.VMEM((num_off, slots, lines, block_rows), jnp.float32),
            pltpu.SMEM((num_off, 1, slots), jnp.int32),
            pltpu.SMEM((1, num_off), jnp.int32),
            pltpu.SemaphoreType.DMA((FLUX_CHUNKS + 3,)),
            pltpu.SemaphoreType.DMA((num_off,)),
            pltpu.SemaphoreType.DMA((chunks * num_off,)),
            pltpu.SemaphoreType.DMA,
            pltpu.SemaphoreType.DMA((num_off - 1,)),
            pltpu.SemaphoreType.DMA((num_off - 1,)),
            pltpu.SemaphoreType.DMA((sends,)),
            pltpu.SemaphoreType.DMA((sends,)),
            pltpu.SemaphoreType.DMA((num_off,)),
            pltpu.SemaphoreType.DMA((num_off,)),
        ],
        compiler_params=pltpu.CompilerParams(
            collective_id=0, has_side_effects=True, vmem_limit_bytes=40 * 1024 * 1024
        ),
    )(*(
        pltpu.with_memory_space_constraint(value, pltpu.HBM)
        for value in (tile_flux, tile_frac, weights[0], block_row.transpose(1, 0, 2), block_col.transpose(1, 0, 2), send_counts)
    ))
    settled = pl.pallas_call(
        settle_kernel,
        out_shape=jax.ShapeDtypeStruct((num_kind, num_step, AB_DEV * block_rows), jnp.float32),
        in_specs=[pl.BlockSpec(memory_space=pltpu.SMEM), pl.BlockSpec(memory_space=pltpu.VMEM)],
        out_specs=pl.BlockSpec(memory_space=pltpu.HBM),
        scratch_shapes=[
            pltpu.VMEM((AB_DEV, lines, block_rows), jnp.float32),
            pltpu.VMEM((num_kind, num_step, AB_DEV * block_rows), jnp.float32),
            pltpu.SemaphoreType.DMA((4,)),
        ],
        compiler_params=pltpu.CompilerParams(vmem_limit_bytes=24 * 1024 * 1024),
    )(tables, arrived)
    return settled.transpose(1, 0, 2)


def solution(mesh):
    sizes = (mesh.shape["gx"], mesh.shape["gy"])
    return jax.shard_map(
        functools.partial(on_device, sizes),
        mesh=mesh,
        in_specs=(
            P(None, None, None, ("gx", "gy")),
            P(None, ("gx", "gy")),
            P(("gx", "gy"), None, None, None, None),
            P(("gx", "gy"), None, None),
            P(("gx", "gy"), None, None),
            P(("gx", "gy"), None),
        ),
        out_specs=P(None, None, ("gx", "gy")),
        check_vma=False,
    )
```

time: 76.6 us -> 68.3 us (0.89)
  local copies, waits for them, and re-layouts: 4.15 us -> 0 us
  Pallas kernels: 72.3 us -> 68.2 us
    unnamed x7 -> x0, local copies, waits for them, and re-layouts: 4.15 us -> none
    pallas_call x1, Pallas kernels: 67.8 us -> 64.8 us  [on_device(): pl.pallas_call(functools.partial(send_kernel, sizes), out_shape=(jax.Shap...]
    pallas_call x1, Pallas kernels: 4.55 us -> 3.45 us  [on_device(): pl.pallas_call(settle_kernel, out_shape=jax.ShapeDtypeStruct((num_kind, n...]
where the time goes in v2:
time: 68.3 us; the launch traced here: 68.2 us
  Pallas kernels  68.2 us (100%)
    pallas_call x1, Pallas kernels, on_device(): pl.pallas_call(functools.partial(send_kernel, sizes), out_shape=(jax.Shap...  64.8 us
    pallas_call x1, Pallas kernels, on_device(): pl.pallas_call(settle_kernel, out_shape=jax.ShapeDtypeStruct((num_kind, n...  3.45 us

profile of v2, /device:TPU:1, one launch (start us, length us, event | category | flops | bytes accessed | tf_op | source)
XLA Modules:
  0.0 68.2 jit_solution(1810367833913410475)
XLA Ops:
  0.0 64.8 %shard_map.64 = (f32[7,16,48,256]{3,2,1,0:T(8,128)S(1)}, s32[7,7,1,16]{3,2,1,0:T(1,128)S(1)}) custom-call(bf16[4,12,32,8,128]{4,3,2,1,0:T(8,128)(2,1)} %bitcast.11, f32[32,8,128]{2,1,0:T(8,128)} %bitcast.12, bf16[7,16,256,128]{3,2,1,0:T(8,128)(2,1)} %bitcast.10, s32[7,1,16]{2,1,0:T(1,128)} %bitcast.13, s32[7,1,16]{2,1,0:T(1,128)} %bitcast.14, s32[1,7]{1,0:T(1,128)} %count_hbm.1), custom_call_target="tpu_custom_call" | custom-call | tf_op jit(solution)/shard_map/pallas_call | solution.py:258
  64.8 3.4 %shard_map.65 = f32[12,4,12288]{2,1,0:T(4,128)} custom-call(s32[7,7,1,16]{3,2,1,0:T(1,128)S(1)} %get-tuple-element.7.table_ref, f32[7,16,48,256]{3,2,1,0:T(8,128)S(1)} %get-tuple-element.8.arrived_ref), custom_call_target="tpu_custom_call" | custom-call | tf_op jit(solution)/shard_map/pallas_call | solution.py:292

commit v3 on v2

v3 whole, which is shorter than its diff:
```python
import functools

import jax
import jax.numpy as jnp
from jax import lax
from jax.experimental import pallas as pl
from jax.experimental.pallas import tpu as pltpu
from jax.sharding import PartitionSpec as P

MESH = pl.DeviceIdType.MESH
AB_DEV = 48
CHUNK = 3
PIECE = 8


def combine(a, b, shift, mask):
    return jnp.where(mask, a + pltpu.roll(a, 8 - shift, 0), b + pltpu.roll(b, shift, 0))


def sum_rows(parts):
    row = lax.broadcasted_iota(jnp.int32, (8, 128), 0)
    top = [combine(parts[r], parts[r + 4], 4, row < 4) for r in range(4)]
    mid = [combine(top[r], top[r + 2], 2, (row & 2) == 0) for r in range(2)]
    return combine(mid[0], mid[1], 1, (row & 1) == 0)


def send_kernel(
    sizes,
    flux_hbm, frac_hbm, weights_hbm, rows_hbm, col_hbm, count_hbm,
    late_hbm, total_hbm, tables_hbm,
    flux_refs, frac_ref, weights_ref, merged_ref, staged_ref, arrived_ref, sums_ref, total_ref,
    col_ref, count_ref, table_ref,
    in_sem, first_weight, weight_sem, total_sem, first_send, first_recv, send_sem, recv_sem, table_send, table_recv, ready_sem,
):
    num_x, num_y = sizes
    devices = num_x * num_y
    pieces = len(flux_refs)
    num_step, piece_kinds = flux_refs[0].shape[:2]
    num_kind = pieces * piece_kinds
    num_off, slots = weights_ref.shape[:2]
    reach = num_off // 2
    others = num_off - 1
    land_blocks = merged_ref.shape[0]
    chunks = (slots - 1) // CHUNK
    sends = chunks * others
    early = sends - others
    atm_blocks = sums_ref.shape[0]
    block_rows = staged_ref.shape[3]
    me = lax.axis_index("gx") * num_y + lax.axis_index("gy")

    def flux_copy(piece):
        kinds = pl.ds(piece * piece_kinds, piece_kinds)
        return pltpu.make_async_copy(flux_hbm.at[:, kinds], flux_refs[piece], in_sem.at[piece])

    def offset_of(turn):
        return (reach - turn // 2) * (1 - 2 * (turn % 2))

    def plan(i):
        return i // others, offset_of(i % others)

    def chunk_part(chunk, offset):
        return offset, pl.ds(1 + chunk * CHUNK, CHUNK)

    def weight_copy(part, sem):
        return pltpu.make_async_copy(weights_hbm.at[part], weights_ref.at[part], sem)

    def first_part(offset):
        return offset, pl.ds(0, 1)

    def target(off):
        there = (me + off + devices) % devices
        return (there // num_y, there % num_y)

    col_copy = pltpu.make_async_copy(col_hbm, col_ref, in_sem.at[pieces + 1])
    count_copy = pltpu.make_async_copy(count_hbm, count_ref, in_sem.at[pieces + 2])
    frac_copy = pltpu.make_async_copy(frac_hbm, frac_ref, in_sem.at[pieces])
    col_copy.start()
    count_copy.start()
    frac_copy.start()
    for offset in range(num_off):
        weight_copy(first_part(offset), first_weight.at[offset]).start()
    for piece in range(pieces):
        flux_copy(piece).start()

    barrier = pltpu.get_barrier_semaphore()
    for step in range(1, reach + 1):
        pl.semaphore_signal(barrier, inc=1, device_id=target(-step), device_id_type=MESH)

    def merge_piece(block, piece, frac, total):
        parts = []
        for line in range(PIECE):
            kind, step = line // num_step, line % num_step
            parts.append(flux_refs[piece][step, kind, block].astype(jnp.float32) * frac)
        return sum_rows(parts) / total

    def merge(block):
        frac = frac_ref[block]
        total = jnp.sum(frac, axis=0, keepdims=True)
        return jnp.concatenate(
            [merge_piece(block, piece, frac, total) for piece in range(pieces)], axis=0
        ).astype(jnp.bfloat16)

    def table_copy(off):
        return pltpu.make_async_remote_copy(
            src_ref=rows_hbm.at[off + reach],
            dst_ref=tables_hbm.at[off + reach],
            send_sem=table_send.at[off + reach],
            recv_sem=table_recv.at[off + reach],
            device_id=target(off),
            device_id_type=MESH,
        )

    def remote(part, off, to_sem, from_sem):
        return pltpu.make_async_remote_copy(
            src_ref=staged_ref.at[part],
            dst_ref=arrived_ref.at[part],
            send_sem=to_sem,
            recv_sem=from_sem,
            device_id=target(off),
            device_id_type=MESH,
        )

    def first_copy(turn):
        off = offset_of(turn)
        return remote(first_part(off + reach), off, first_send.at[turn], first_recv.at[turn])

    def chunk_copy(i):
        chunk, off = plan(i)
        return remote(chunk_part(chunk, off + reach), off, send_sem.at[i], recv_sem.at[i])

    def late_copy(turn):
        off = offset_of(turn)
        return pltpu.make_async_remote_copy(
            src_ref=staged_ref.at[chunk_part(chunks - 1, off + reach)],
            dst_ref=late_hbm.at[turn],
            send_sem=send_sem.at[early + turn],
            recv_sem=recv_sem.at[early + turn],
            device_id=target(off),
            device_id_type=MESH,
        )

    def product(picked, offset, slot):
        picked = jnp.where(slot < count_ref[0, offset], picked, jnp.zeros_like(picked))
        return lax.dot_general(
            picked, weights_ref[offset, slot], (((1,), (1,)), ((), ())),
            preferred_element_type=jnp.float32,
        )

    def multiply(picked, offset, slot):
        staged_ref[offset, slot] = product(picked, offset, slot)

    def multiply_chunk(chunk, offset):
        for step in range(CHUNK):
            slot = 1 + chunk * CHUNK + step
            multiply(merged_ref[col_ref[offset, 0, slot]], offset, slot)

    pl.semaphore_wait(barrier, reach)
    for step in range(1, reach + 1):
        pl.semaphore_signal(ready_sem, inc=1, device_id=target(step), device_id_type=MESH)

    col_copy.wait()
    count_copy.wait()
    frac_copy.wait()
    for offset in range(num_off):
        if offset != reach:
            weight_copy(first_part(offset), first_weight.at[offset]).wait()
    for piece in range(pieces):
        flux_copy(piece).wait()
        lines = pl.ds(piece * PIECE, PIECE)
        for off in list(range(reach, 0, -1)) + list(range(-reach, 0)):
            block = col_ref[off + reach, 0, 0]
            frac = frac_ref[block]
            picked = merge_piece(block, piece, frac, jnp.sum(frac, axis=0, keepdims=True))
            staged_ref[off + reach, 0, lines, :] = product(picked.astype(jnp.bfloat16), off + reach, 0)
        for off in range(reach, 0, -1):
            remote(
                (off + reach, 0, lines), off, first_send.at[2 * (reach - off)], first_recv.at[2 * (reach - off)]
            ).start()

    @pl.loop(0, sends)
    def _(i):
        chunk, off = plan(i)
        weight_copy(chunk_part(chunk, off + reach), weight_sem.at[i]).start()

    @pl.loop(0, chunks)
    def _(chunk):
        weight_copy(chunk_part(chunk, reach), weight_sem.at[sends + chunk]).start()

    pl.semaphore_wait(ready_sem, reach)
    for turn in range(1, others, 2):
        first_copy(turn).start()
    for off in range(-reach, reach + 1):
        if off:
            table_copy(off).start()

    @pl.loop(0, land_blocks)
    def _(block):
        merged_ref[block] = merge(block)

    @pl.loop(0, sends)
    def _(i):
        chunk, off = plan(i)
        weight_copy(chunk_part(chunk, off + reach), weight_sem.at[i]).wait()
        multiply_chunk(chunk, off + reach)

        @pl.when(jnp.logical_and(i > 0, i <= early))
        def _():
            chunk_copy(i - 1).start()

        @pl.when(i > early)
        def _():
            late_copy(i - 1 - early).start()

    own_table = pltpu.make_async_copy(rows_hbm.at[reach], tables_hbm.at[reach], in_sem.at[0])
    own_table.start()
    weight_copy(first_part(reach), first_weight.at[reach]).wait()
    multiply(merged_ref[col_ref[reach, 0, 0]], reach, 0)
    late_copy(others - 1).start()

    @pl.loop(0, chunks)
    def _(chunk):
        weight_copy(chunk_part(chunk, reach), weight_sem.at[sends + chunk]).wait()
        multiply_chunk(chunk, reach)

    for off in range(-reach, reach + 1):
        if off:
            table_copy(off).wait()
    own_table.wait()
    all_tables = pltpu.make_async_copy(tables_hbm, table_ref, in_sem.at[1])
    all_tables.start()
    all_tables.wait()

    def accumulate(block, start, slots_in):
        total = start
        for ref, offset, slot in slots_in:
            here = table_ref[offset, 0, slot] == block
            value = ref[offset, slot]
            total = total + jnp.where(here, value, jnp.zeros_like(value))
        sums_ref[block] = total

    @pl.loop(0, atm_blocks)
    def _(block):
        accumulate(
            block,
            jnp.zeros(sums_ref.shape[1:], jnp.float32),
            [(staged_ref, reach, slot) for slot in range(slots)],
        )

    @pl.loop(0, others)
    def _(turn):
        first_copy(turn).wait()

    @pl.loop(0, atm_blocks)
    def _(block):
        accumulate(
            block, sums_ref[block], [(arrived_ref, offset, 0) for offset in range(num_off) if offset != reach]
        )

    @pl.loop(0, chunks - 1)
    def _(chunk):
        @pl.loop(0, others)
        def _(turn):
            chunk_copy(chunk * others + turn).wait_recv()

        @pl.loop(0, atm_blocks)
        def _(block):
            accumulate(
                block,
                sums_ref[block],
                [
                    (arrived_ref, offset, 1 + chunk * CHUNK + step)
                    for offset in range(num_off)
                    if offset != reach
                    for step in range(CHUNK)
                ],
            )

    @pl.loop(0, atm_blocks, unroll=2)
    def _(block):
        cells = pl.ds(pl.multiple_of(block * block_rows, block_rows), block_rows)
        for kind in range(num_kind):
            total_ref[kind, :, cells] = sums_ref[block, pl.ds(kind * num_step, num_step), :]

    total_out = pltpu.make_async_copy(total_ref, total_hbm, total_sem)
    total_out.start()

    @pl.loop(0, early)
    def _(i):
        chunk_copy(i).wait_send()

    total_out.wait()

    @pl.loop(0, others)
    def _(turn):
        late_copy(turn).wait()


def settle_kernel(table_ref, late_ref, total_ref, out_hbm, out_ref, touched_ref, out_sem):
    others, steps, _, block_rows = late_ref.shape
    num_kind, num_step, cells_dev = out_ref.shape
    atm_blocks = cells_dev // block_rows
    reach = others // 2
    first_slot = table_ref.shape[2] - steps

    def cells_of(block):
        return pl.ds(pl.multiple_of(block * block_rows, block_rows), block_rows)

    def emit(ref, block):
        cells = cells_of(block)
        return pltpu.make_async_copy(ref.at[:, :, cells], out_hbm.at[:, :, cells], out_sem)

    arrivals = []
    for turn in range(others):
        offset = (reach - turn // 2) * (1 - 2 * (turn % 2)) + reach
        arrivals += [(turn, step, offset) for step in range(steps)]

    @pl.loop(0, atm_blocks, unroll=8)
    def _(block):
        touched_ref[block] = 0

    for turn, step, offset in arrivals:
        touched_ref[table_ref[offset, 0, first_slot + step]] = 1

    @pl.loop(0, atm_blocks)
    def _(block):
        @pl.when(touched_ref[block] == 0)
        def _():
            emit(total_ref, block).start()

    for turn, step, offset in arrivals:
        block = table_ref[offset, 0, first_slot + step]
        cells = cells_of(block)
        fresh = touched_ref[block] == 1
        touched_ref[block] = 2

        @pl.when(fresh)
        def _():
            for kind in range(num_kind):
                out_ref[kind, :, cells] = (
                    total_ref[kind, :, cells] + late_ref[turn, step, pl.ds(kind * num_step, num_step), :]
                )

        @pl.when(jnp.logical_not(fresh))
        def _():
            for kind in range(num_kind):
                out_ref[kind, :, cells] = (
                    out_ref[kind, :, cells] + late_ref[turn, step, pl.ds(kind * num_step, num_step), :]
                )

    @pl.loop(0, atm_blocks)
    def _(block):
        @pl.when(touched_ref[block] == 2)
        def _():
            emit(out_ref, block).start()

    pltpu.make_async_copy(total_ref, out_hbm, out_sem).wait()


def on_device(sizes, tile_flux, tile_frac, weights, block_row, block_col, send_counts):
    num_step, num_kind, tiles, cells = tile_flux.shape
    num_off, slots, block_rows, block_cols = weights.shape[1:]
    lines = num_step * num_kind
    chunks = (slots - 1) // CHUNK
    sends = chunks * (num_off - 1)
    tile_flux = tile_flux.reshape(num_step, num_kind, tiles, -1, block_cols).transpose(0, 1, 3, 2, 4)
    tile_frac = tile_frac.reshape(tiles, -1, block_cols).transpose(1, 0, 2)
    late, total, tables = pl.pallas_call(
        functools.partial(send_kernel, sizes),
        out_shape=(
            jax.ShapeDtypeStruct((num_off - 1, CHUNK, lines, block_rows), jnp.float32),
            jax.ShapeDtypeStruct((num_kind, num_step, AB_DEV * block_rows), jnp.float32),
            jax.ShapeDtypeStruct((num_off, 1, slots), jnp.int32),
        ),
        in_specs=[pl.BlockSpec(memory_space=pltpu.HBM)] * 6,
        out_specs=(pl.BlockSpec(memory_space=pl.ANY),) * 3,
        scratch_shapes=[
            [pltpu.VMEM((num_step, PIECE // num_step) + tile_flux.shape[2:], jnp.bfloat16)] * (lines // PIECE),
            pltpu.VMEM(tile_frac.shape, jnp.float32),
            pltpu.VMEM(weights.shape[1:], jnp.bfloat16),
            pltpu.VMEM((cells // block_cols, lines, block_cols), jnp.bfloat16),
            pltpu.VMEM((num_off, slots, lines, block_rows), jnp.float32),
            pltpu.VMEM((num_off, slots, lines, block_rows), jnp.float32),
            pltpu.VMEM((AB_DEV, lines, block_rows), jnp.float32),
            pltpu.VMEM((num_kind, num_step, AB_DEV * block_rows), jnp.float32),
            pltpu.SMEM((num_off, 1, slots), jnp.int32),
            pltpu.SMEM((1, num_off), jnp.int32),
            pltpu.SMEM((num_off, 1, slots), jnp.int32),
            pltpu.SemaphoreType.DMA((lines // PIECE + 3,)),
            pltpu.SemaphoreType.DMA((num_off,)),
            pltpu.SemaphoreType.DMA((chunks * num_off,)),
            pltpu.SemaphoreType.DMA,
            pltpu.SemaphoreType.DMA((num_off - 1,)),
            pltpu.SemaphoreType.DMA((num_off - 1,)),
            pltpu.SemaphoreType.DMA((sends,)),
            pltpu.SemaphoreType.DMA((sends,)),
            pltpu.SemaphoreType.DMA((num_off,)),
            pltpu.SemaphoreType.DMA((num_off,)),
            pltpu.SemaphoreType.REGULAR,
        ],
        compiler_params=pltpu.CompilerParams(
            collective_id=0, has_side_effects=True, vmem_limit_bytes=40 * 1024 * 1024
        ),
    )(*(
        pltpu.with_memory_space_constraint(value, pltpu.HBM)
        for value in (tile_flux, tile_frac, weights[0], block_row.transpose(1, 0, 2), block_col.transpose(1, 0, 2), send_counts)
    ))
    settled = pl.pallas_call(
        settle_kernel,
        out_shape=jax.ShapeDtypeStruct((num_kind, num_step, AB_DEV * block_rows), jnp.float32),
        in_specs=[pl.BlockSpec(memory_space=pltpu.SMEM)] + [pl.BlockSpec(memory_space=pltpu.VMEM)] * 2,
        out_specs=pl.BlockSpec(memory_space=pltpu.HBM),
        scratch_shapes=[
            pltpu.VMEM((num_kind, num_step, AB_DEV * block_rows), jnp.float32),
            pltpu.SMEM((AB_DEV,), jnp.int32),
            pltpu.SemaphoreType.DMA,
        ],
        compiler_params=pltpu.CompilerParams(vmem_limit_bytes=12 * 1024 * 1024),
    )(tables, late, total)
    return settled.transpose(1, 0, 2)


def solution(mesh):
    sizes = (mesh.shape["gx"], mesh.shape["gy"])
    return jax.shard_map(
        functools.partial(on_device, sizes),
        mesh=mesh,
        in_specs=(
            P(None, None, None, ("gx", "gy")),
            P(None, ("gx", "gy")),
            P(("gx", "gy"), None, None, None, None),
            P(("gx", "gy"), None, None),
            P(("gx", "gy"), None, None),
            P(("gx", "gy"), None),
        ),
        out_specs=P(None, None, ("gx", "gy")),
        check_vma=False,
    )
```

time: 68.3 us -> 67.6 us (0.990)
  Pallas kernels: 68.2 us -> 67.5 us
    pallas_call x1, Pallas kernels: 3.45 us -> 2.52 us  [on_device(): pl.pallas_call(settle_kernel, out_shape=jax.ShapeDtypeStruct((num_kind, n...]
where the time goes in v3:
time: 67.6 us; the launch traced here: 67.5 us
  Pallas kernels  67.5 us (100%)
    pallas_call x1, Pallas kernels, on_device(): pl.pallas_call(functools.partial(send_kernel, sizes), out_shape=(jax.Shap...  65 us
    pallas_call x1, Pallas kernels, on_device(): pl.pallas_call(settle_kernel, out_shape=jax.ShapeDtypeStruct((num_kind, n...  2.52 us

profile of v3, /device:TPU:1, one launch (start us, length us, event | category | flops | bytes accessed | tf_op | source)
XLA Modules:
  0.0 67.5 jit_solution(14439229928555073734)
XLA Ops:
  0.0 65.0 %shard_map.64 = (f32[6,3,48,256]{3,2,1,0:T(8,128)S(1)}, f32[12,4,12288]{2,1,0:T(4,128)S(1)}, s32[7,1,16]{2,1,0:T(1,128)S(1)}) custom-call(bf16[4,12,32,8,128]{4,3,2,1,0:T(8,128)(2,1)} %bitcast.11, f32[32,8,128]{2,1,0:T(8,128)} %bitcast.12, bf16[7,16,256,128]{3,2,1,0:T(8,128)(2,1)} %bitcast.10, s32[7,1,16]{2,1,0:T(1,128)} %bitcast.13, s32[7,1,16]{2,1,0:T(1,128)} %bitcast.14, ...), custom_call_target="tpu_custom_call" | custom-call | tf_op jit(solution)/shard_map/pallas_call | solution.py:367
  65.0 2.5 %shard_map.65 = f32[12,4,12288]{2,1,0:T(4,128)} custom-call(s32[7,1,16]{2,1,0:T(1,128)S(1)} %get-tuple-element.8.table_ref, f32[6,3,48,256]{3,2,1,0:T(8,128)S(1)} %get-tuple-element.9.late_ref, f32[12,4,12288]{2,1,0:T(4,128)S(1)} %get-tuple-element.10.total_ref), custom_call_target="tpu_custom_call" | custom-call | tf_op jit(solution)/shard_map/pallas_call | solution.py:407

commit v4 on v3

--- a/solution.py
+++ b/solution.py
@@ -67,6 +67,9 @@
     def first_part(offset):
         return offset, pl.ds(0, 1)
 
+    def rest_copy(offset):
+        return weight_copy((offset, pl.ds(1, slots - 1)), weight_sem.at[offset])
+
     def target(off):
         there = (me + off + devices) % devices
         return (there // num_y, there % num_y)
@@ -176,15 +179,14 @@
             remote(
                 (off + reach, 0, lines), off, first_send.at[2 * (reach - off)], first_recv.at[2 * (reach - off)]
             ).start()
-
-    @pl.loop(0, sends)
-    def _(i):
-        chunk, off = plan(i)
-        weight_copy(chunk_part(chunk, off + reach), weight_sem.at[i]).start()
-
-    @pl.loop(0, chunks)
-    def _(chunk):
-        weight_copy(chunk_part(chunk, reach), weight_sem.at[sends + chunk]).start()
+        if piece == pieces // 2:
+            for turn in range(others):
+                rest_copy(offset_of(turn) + reach).start()
+            rest_copy(reach).start()
+
+    @pl.loop(0, land_blocks)
+    def _(block):
+        merged_ref[block] = merge(block)
 
     pl.semaphore_wait(ready_sem, reach)
     for turn in range(1, others, 2):
@@ -193,14 +195,14 @@
         if off:
             table_copy(off).start()
 
-    @pl.loop(0, land_blocks)
-    def _(block):
-        merged_ref[block] = merge(block)
-
     @pl.loop(0, sends)
     def _(i):
         chunk, off = plan(i)
-        weight_copy(chunk_part(chunk, off + reach), weight_sem.at[i]).wait()
+
+        @pl.when(i < others)
+        def _():
+            rest_copy(off + reach).wait()
+
         multiply_chunk(chunk, off + reach)
 
         @pl.when(jnp.logical_and(i > 0, i <= early))
@@ -217,9 +219,10 @@
     multiply(merged_ref[col_ref[reach, 0, 0]], reach, 0)
     late_copy(others - 1).start()
 
+    rest_copy(reach).wait()
+
     @pl.loop(0, chunks)
     def _(chunk):
-        weight_copy(chunk_part(chunk, reach), weight_sem.at[sends + chunk]).wait()
         multiply_chunk(chunk, reach)
 
     for off in range(-reach, reach + 1):
@@ -387,7 +390,7 @@
             pltpu.SMEM((num_off, 1, slots), jnp.int32),
             pltpu.SemaphoreType.DMA((lines // PIECE + 3,)),
             pltpu.SemaphoreType.DMA((num_off,)),
-            pltpu.SemaphoreType.DMA((chunks * num_off,)),
+            pltpu.SemaphoreType.DMA((num_off,)),
             pltpu.SemaphoreType.DMA,
             pltpu.SemaphoreType.DMA((num_off - 1,)),
             pltpu.SemaphoreType.DMA((num_off - 1,)),

time: 67.6 us -> 66.7 us (0.987)
  Pallas kernels: 67.5 us -> 66.7 us
    pallas_call x1, Pallas kernels: 65 us -> 64.1 us  [on_device(): pl.pallas_call(functools.partial(send_kernel, sizes), out_shape=(jax.Shap...]
where the time goes in v4:
time: 66.7 us
  Pallas kernels  66.7 us (100%)
    pallas_call x1, Pallas kernels, on_device(): pl.pallas_call(functools.partial(send_kernel, sizes), out_shape=(jax.Shap...  64.1 us
    pallas_call x1, Pallas kernels, on_device(): pl.pallas_call(settle_kernel, out_shape=jax.ShapeDtypeStruct((num_kind, n...  2.53 us

profile of v4, /device:TPU:1, one launch (start us, length us, event | category | flops | bytes accessed | tf_op | source)
XLA Modules:
  0.0 66.7 jit_solution(14505907114142880732)
XLA Ops:
  0.0 64.1 %shard_map.64 = (f32[6,3,48,256]{3,2,1,0:T(8,128)S(1)}, f32[12,4,12288]{2,1,0:T(4,128)S(1)}, s32[7,1,16]{2,1,0:T(1,128)S(1)}) custom-call(bf16[4,12,32,8,128]{4,3,2,1,0:T(8,128)(2,1)} %bitcast.11, f32[32,8,128]{2,1,0:T(8,128)} %bitcast.12, bf16[7,16,256,128]{3,2,1,0:T(8,128)(2,1)} %bitcast.10, s32[7,1,16]{2,1,0:T(1,128)} %bitcast.13, s32[7,1,16]{2,1,0:T(1,128)} %bitcast.14, ...), custom_call_target="tpu_custom_call" | custom-call | tf_op jit(solution)/shard_map/pallas_call | solution.py:370
  64.1 2.5 %shard_map.65 = f32[12,4,12288]{2,1,0:T(4,128)} custom-call(s32[7,1,16]{2,1,0:T(1,128)S(1)} %get-tuple-element.8.table_ref, f32[6,3,48,256]{3,2,1,0:T(8,128)S(1)} %get-tuple-element.9.late_ref, f32[12,4,12288]{2,1,0:T(4,128)S(1)} %get-tuple-element.10.total_ref), custom_call_target="tpu_custom_call" | custom-call | tf_op jit(solution)/shard_map/pallas_call | solution.py:410

commit v5 on v4

--- a/solution.py
+++ b/solution.py
@@ -11,6 +11,9 @@
 AB_DEV = 48
 CHUNK = 3
 PIECE = 8
+COLUMN = 16
+RELAYED = 2
+HELP_AT = 10
 
 
 def combine(a, b, shift, mask):
@@ -31,6 +34,7 @@
     flux_refs, frac_ref, weights_ref, merged_ref, staged_ref, arrived_ref, sums_ref, total_ref,
     col_ref, count_ref, table_ref,
     in_sem, first_weight, weight_sem, total_sem, first_send, first_recv, send_sem, recv_sem, table_send, table_recv, ready_sem,
+    relay_ref, relay_ready, relay_send, relay_recv, pass_send, pass_recv,
 ):
     num_x, num_y = sizes
     devices = num_x * num_y
@@ -48,6 +52,16 @@
     block_rows = staged_ref.shape[3]
     me = lax.axis_index("gx") * num_y + lax.axis_index("gy")
 
+    columns = num_y // COLUMN
+    my_column = lax.axis_index("gy") // COLUMN
+    my_chip = lax.axis_index("gy") % COLUMN // 2
+    at_end = my_chip == COLUMN // 2 - 1
+    is_source = jnp.logical_and(at_end, my_column == columns - 1)
+    is_helper = jnp.logical_and(at_end, my_column < columns - 1)
+    is_receiver = jnp.logical_and(my_chip == 0, my_column == 0)
+    helpers = columns - 1
+    assert helpers == CHUNK
+
     def flux_copy(piece):
         kinds = pl.ds(piece * piece_kinds, piece_kinds)
         return pltpu.make_async_copy(flux_hbm.at[:, kinds], flux_refs[piece], in_sem.at[piece])
@@ -73,6 +87,29 @@
     def target(off):
         there = (me + off + devices) % devices
         return (there // num_y, there % num_y)
+
+    relay_off = 2
+    relay_at = relay_off + reach
+
+    def relay_copy(helper):
+        return pltpu.make_async_remote_copy(
+            src_ref=staged_ref.at[relay_at, 1 + helper],
+            dst_ref=relay_ref,
+            send_sem=relay_send.at[helper],
+            recv_sem=relay_recv,
+            device_id=target(-COLUMN * (helpers - helper)),
+            device_id_type=MESH,
+        )
+
+    def pass_copy(helper):
+        return pltpu.make_async_remote_copy(
+            src_ref=relay_ref,
+            dst_ref=arrived_ref.at[relay_at, 1 + helper],
+            send_sem=pass_send,
+            recv_sem=pass_recv.at[helper],
+            device_id=target(COLUMN * (helpers - helper) + relay_off),
+            device_id_type=MESH,
+        )
 
     col_copy = pltpu.make_async_copy(col_hbm, col_ref, in_sem.at[pieces + 1])
     count_copy = pltpu.make_async_copy(count_hbm, count_ref, in_sem.at[pieces + 2])
@@ -89,6 +126,20 @@
     for step in range(1, reach + 1):
         pl.semaphore_signal(barrier, inc=1, device_id=target(-step), device_id_type=MESH)
 
+    @pl.when(is_source)
+    def _():
+        for helper in range(helpers):
+            pl.semaphore_signal(
+                barrier, inc=1, device_id=target(-COLUMN * (helpers - helper)), device_id_type=MESH
+            )
+
+    @pl.when(is_receiver)
+    def _():
+        for helper in range(helpers):
+            pl.semaphore_signal(
+                barrier, inc=1, device_id=target(-relay_off - COLUMN * (helpers - helper)), device_id_type=MESH
+            )
+
     def merge_piece(block, piece, frac, total):
         parts = []
         for line in range(PIECE):
@@ -157,7 +208,17 @@
             slot = 1 + chunk * CHUNK + step
             multiply(merged_ref[col_ref[offset, 0, slot]], offset, slot)
 
-    pl.semaphore_wait(barrier, reach)
+    @pl.when(jnp.logical_not(is_helper))
+    def _():
+        pl.semaphore_wait(barrier, reach)
+
+    @pl.when(is_helper)
+    def _():
+        pl.semaphore_wait(barrier, reach + 2)
+        pl.semaphore_signal(
+            relay_ready, inc=1, device_id=target(COLUMN * (helpers - my_column)), device_id_type=MESH
+        )
+
     for step in range(1, reach + 1):
         pl.semaphore_signal(ready_sem, inc=1, device_id=target(step), device_id_type=MESH)
 
@@ -205,9 +266,22 @@
 
         multiply_chunk(chunk, off + reach)
 
-        @pl.when(jnp.logical_and(i > 0, i <= early))
+        relayed = jnp.logical_and(is_source, i == RELAYED + 1)
+
+        @pl.when(jnp.logical_and(jnp.logical_and(i > 0, i <= early), jnp.logical_not(relayed)))
         def _():
             chunk_copy(i - 1).start()
+
+        @pl.when(relayed)
+        def _():
+            pl.semaphore_wait(relay_ready, helpers)
+            for helper in range(helpers):
+                relay_copy(helper).start()
+
+        @pl.when(jnp.logical_and(is_helper, i == HELP_AT))
+        def _():
+            relay_copy(0).wait_recv()
+            pass_copy(my_column).start()
 
         @pl.when(i > early)
         def _():
@@ -263,7 +337,14 @@
     def _(chunk):
         @pl.loop(0, others)
         def _(turn):
-            chunk_copy(chunk * others + turn).wait_recv()
+            @pl.when(jnp.logical_not(jnp.logical_and(is_receiver, chunk * others + turn == RELAYED)))
+            def _():
+                chunk_copy(chunk * others + turn).wait_recv()
+
+        @pl.when(jnp.logical_and(is_receiver, chunk == 0))
+        def _():
+            for helper in range(helpers):
+                pass_copy(helper).wait_recv()
 
         @pl.loop(0, atm_blocks)
         def _(block):
@@ -289,7 +370,18 @@
 
     @pl.loop(0, early)
     def _(i):
-        chunk_copy(i).wait_send()
+        @pl.when(jnp.logical_not(jnp.logical_and(is_source, i == RELAYED)))
+        def _():
+            chunk_copy(i).wait_send()
+
+    @pl.when(is_source)
+    def _():
+        for helper in range(helpers):
+            relay_copy(helper).wait_send()
+
+    @pl.when(is_helper)
+    def _():
+        pass_copy(my_column).wait_send()
 
     total_out.wait()
 
@@ -399,6 +491,12 @@
             pltpu.SemaphoreType.DMA((num_off,)),
             pltpu.SemaphoreType.DMA((num_off,)),
             pltpu.SemaphoreType.REGULAR,
+            pltpu.VMEM((lines, block_rows), jnp.float32),
+            pltpu.SemaphoreType.REGULAR,
+            pltpu.SemaphoreType.DMA((CHUNK,)),
+            pltpu.SemaphoreType.DMA,
+            pltpu.SemaphoreType.DMA,
+            pltpu.SemaphoreType.DMA((CHUNK,)),
         ],
         compiler_params=pltpu.CompilerParams(
             collective_id=0, has_side_effects=True, vmem_limit_bytes=40 * 1024 * 1024

time: 66.7 us -> 65 us (0.975)
  Pallas kernels: 66.7 us -> 64.6 us
    pallas_call x1, Pallas kernels: 64.1 us -> 62.1 us  [on_device(): pl.pallas_call(functools.partial(send_kernel, sizes), out_shape=(jax.Shap...]
where the time goes in v5:
time: 65 us; the launch traced here: 64.6 us
  Pallas kernels  64.6 us (99%)
    pallas_call x1, Pallas kernels, on_device(): pl.pallas_call(functools.partial(send_kernel, sizes), out_shape=(jax.Shap...  62.1 us
    pallas_call x1, Pallas kernels, on_device(): pl.pallas_call(settle_kernel, out_shape=jax.ShapeDtypeStruct((num_kind, n...  2.48 us

profile of v5, /device:TPU:1, one launch (start us, length us, event | category | flops | bytes accessed | tf_op | source)
XLA Modules:
  0.0 64.6 jit_solution(3460694220067464151)
XLA Ops:
  0.0 62.1 %shard_map.64 = (f32[6,3,48,256]{3,2,1,0:T(8,128)S(1)}, f32[12,4,12288]{2,1,0:T(4,128)S(1)}, s32[7,1,16]{2,1,0:T(1,128)S(1)}) custom-call(bf16[4,12,32,8,128]{4,3,2,1,0:T(8,128)(2,1)} %bitcast.11, f32[32,8,128]{2,1,0:T(8,128)} %bitcast.12, bf16[7,16,256,128]{3,2,1,0:T(8,128)(2,1)} %bitcast.10, s32[7,1,16]{2,1,0:T(1,128)} %bitcast.13, s32[7,1,16]{2,1,0:T(1,128)} %bitcast.14, ...), custom_call_target="tpu_custom_call" | custom-call | tf_op jit(solution)/shard_map/pallas_call | solution.py:462
  62.1 2.5 %shard_map.65 = f32[12,4,12288]{2,1,0:T(4,128)} custom-call(s32[7,1,16]{2,1,0:T(1,128)S(1)} %get-tuple-element.8.table_ref, f32[6,3,48,256]{3,2,1,0:T(8,128)S(1)} %get-tuple-element.9.late_ref, f32[12,4,12288]{2,1,0:T(4,128)S(1)} %get-tuple-element.10.total_ref), custom_call_target="tpu_custom_call" | custom-call | tf_op jit(solution)/shard_map/pallas_call | solution.py:508

commit v6 on v5

--- a/solution.py
+++ b/solution.py
@@ -32,7 +32,7 @@
     flux_hbm, frac_hbm, weights_hbm, rows_hbm, col_hbm, count_hbm,
     late_hbm, total_hbm, tables_hbm,
     flux_refs, frac_ref, weights_ref, merged_ref, staged_ref, arrived_ref, sums_ref, total_ref,
-    col_ref, count_ref, table_ref,
+    col_ref, count_ref, table_ref, rows_ref, live_rows_ref,
     in_sem, first_weight, weight_sem, total_sem, first_send, first_recv, send_sem, recv_sem, table_send, table_recv, ready_sem,
     relay_ref, relay_ready, relay_send, relay_recv, pass_send, pass_recv,
 ):
@@ -114,6 +114,7 @@
     col_copy = pltpu.make_async_copy(col_hbm, col_ref, in_sem.at[pieces + 1])
     count_copy = pltpu.make_async_copy(count_hbm, count_ref, in_sem.at[pieces + 2])
     frac_copy = pltpu.make_async_copy(frac_hbm, frac_ref, in_sem.at[pieces])
+    rows_copy = pltpu.make_async_copy(rows_hbm, rows_ref, in_sem.at[pieces + 3])
     col_copy.start()
     count_copy.start()
     frac_copy.start()
@@ -121,6 +122,7 @@
         weight_copy(first_part(offset), first_weight.at[offset]).start()
     for piece in range(pieces):
         flux_copy(piece).start()
+    rows_copy.start()
 
     barrier = pltpu.get_barrier_semaphore()
     for step in range(1, reach + 1):
@@ -156,7 +158,7 @@
 
     def table_copy(off):
         return pltpu.make_async_remote_copy(
-            src_ref=rows_hbm.at[off + reach],
+            src_ref=live_rows_ref.at[off + reach],
             dst_ref=tables_hbm.at[off + reach],
             send_sem=table_send.at[off + reach],
             recv_sem=table_recv.at[off + reach],
@@ -245,6 +247,11 @@
                 rest_copy(offset_of(turn) + reach).start()
             rest_copy(reach).start()
 
+    rows_copy.wait()
+    slot_ids = lax.broadcasted_iota(jnp.int32, (1, slots), 1)
+    for offset in range(num_off):
+        live_rows_ref[offset] = jnp.where(slot_ids < count_ref[0, offset], rows_ref[offset], -1)
+
     @pl.loop(0, land_blocks)
     def _(block):
         merged_ref[block] = merge(block)
@@ -287,7 +294,7 @@
         def _():
             late_copy(i - 1 - early).start()
 
-    own_table = pltpu.make_async_copy(rows_hbm.at[reach], tables_hbm.at[reach], in_sem.at[0])
+    own_table = pltpu.make_async_copy(live_rows_ref.at[reach], tables_hbm.at[reach], in_sem.at[0])
     own_table.start()
     weight_copy(first_part(reach), first_weight.at[reach]).wait()
     multiply(merged_ref[col_ref[reach, 0, 0]], reach, 0)
@@ -409,44 +416,62 @@
         offset = (reach - turn // 2) * (1 - 2 * (turn % 2)) + reach
         arrivals += [(turn, step, offset) for step in range(steps)]
 
-    @pl.loop(0, atm_blocks, unroll=8)
-    def _(block):
-        touched_ref[block] = 0
-
+    live = 0
     for turn, step, offset in arrivals:
-        touched_ref[table_ref[offset, 0, first_slot + step]] = 1
-
-    @pl.loop(0, atm_blocks)
-    def _(block):
-        @pl.when(touched_ref[block] == 0)
-        def _():
-            emit(total_ref, block).start()
-
-    for turn, step, offset in arrivals:
-        block = table_ref[offset, 0, first_slot + step]
-        cells = cells_of(block)
-        fresh = touched_ref[block] == 1
-        touched_ref[block] = 2
-
-        @pl.when(fresh)
-        def _():
-            for kind in range(num_kind):
-                out_ref[kind, :, cells] = (
-                    total_ref[kind, :, cells] + late_ref[turn, step, pl.ds(kind * num_step, num_step), :]
-                )
-
-        @pl.when(jnp.logical_not(fresh))
-        def _():
-            for kind in range(num_kind):
-                out_ref[kind, :, cells] = (
-                    out_ref[kind, :, cells] + late_ref[turn, step, pl.ds(kind * num_step, num_step), :]
-                )
-
-    @pl.loop(0, atm_blocks)
-    def _(block):
-        @pl.when(touched_ref[block] == 2)
-        def _():
-            emit(out_ref, block).start()
+        live = live + jnp.where(table_ref[offset, 0, first_slot + step] >= 0, 1, 0)
+
+    @pl.when(live == 0)
+    def _():
+        pltpu.make_async_copy(total_ref, out_hbm, out_sem).start()
+
+    @pl.when(live > 0)
+    def _():
+        @pl.loop(0, atm_blocks, unroll=8)
+        def _(block):
+            touched_ref[block] = 0
+
+        for turn, step, offset in arrivals:
+            row = table_ref[offset, 0, first_slot + step]
+
+            @pl.when(row >= 0)
+            def _():
+                touched_ref[jnp.maximum(row, 0)] = 1
+
+        @pl.loop(0, atm_blocks)
+        def _(block):
+            @pl.when(touched_ref[block] == 0)
+            def _():
+                emit(total_ref, block).start()
+
+        for turn, step, offset in arrivals:
+            row = table_ref[offset, 0, first_slot + step]
+
+            @pl.when(row >= 0)
+            def _():
+                block = jnp.maximum(row, 0)
+                cells = cells_of(block)
+                fresh = touched_ref[block] == 1
+                touched_ref[block] = 2
+
+                @pl.when(fresh)
+                def _():
+                    for kind in range(num_kind):
+                        out_ref[kind, :, cells] = (
+                            total_ref[kind, :, cells] + late_ref[turn, step, pl.ds(kind * num_step, num_step), :]
+                        )
+
+                @pl.when(jnp.logical_not(fresh))
+                def _():
+                    for kind in range(num_kind):
+                        out_ref[kind, :, cells] = (
+                            out_ref[kind, :, cells] + late_ref[turn, step, pl.ds(kind * num_step, num_step), :]
+                        )
+
+        @pl.loop(0, atm_blocks)
+        def _(block):
+            @pl.when(touched_ref[block] == 2)
+            def _():
+                emit(out_ref, block).start()
 
     pltpu.make_async_copy(total_ref, out_hbm, out_sem).wait()
 
@@ -480,7 +505,9 @@
             pltpu.SMEM((num_off, 1, slots), jnp.int32),
             pltpu.SMEM((1, num_off), jnp.int32),
             pltpu.SMEM((num_off, 1, slots), jnp.int32),
-            pltpu.SemaphoreType.DMA((lines // PIECE + 3,)),
+            pltpu.VMEM((num_off, 1, slots), jnp.int32),
+            pltpu.VMEM((num_off, 1, slots), jnp.int32),
+            pltpu.SemaphoreType.DMA((lines // PIECE + 4,)),
             pltpu.SemaphoreType.DMA((num_off,)),
             pltpu.SemaphoreType.DMA((num_off,)),
             pltpu.SemaphoreType.DMA,

time: 65 us -> 64.5 us (level)
  no operation moved by 1% of the time
where the time goes in v6:
time: 64.5 us; the launch traced here: 64.2 us
  Pallas kernels  64.1 us (99%)
    pallas_call x1, Pallas kernels, on_device(): pl.pallas_call(functools.partial(send_kernel, sizes), out_shape=(jax.Shap...  62.1 us
    pallas_call x1, Pallas kernels, on_device(): pl.pallas_call(settle_kernel, out_shape=jax.ShapeDtypeStruct((num_kind, n...  2.03 us

profile of v6, /device:TPU:1, one launch (start us, length us, event | category | flops | bytes accessed | tf_op | source)
XLA Modules:
  0.0 64.2 jit_solution(4583849264817704235)
XLA Ops:
  0.0 62.1 %shard_map.64 = (f32[6,3,48,256]{3,2,1,0:T(8,128)S(1)}, f32[12,4,12288]{2,1,0:T(4,128)S(1)}, s32[7,1,16]{2,1,0:T(1,128)S(1)}) custom-call(bf16[4,12,32,8,128]{4,3,2,1,0:T(8,128)(2,1)} %bitcast.11, f32[32,8,128]{2,1,0:T(8,128)} %bitcast.12, bf16[7,16,256,128]{3,2,1,0:T(8,128)(2,1)} %bitcast.10, s32[7,1,16]{2,1,0:T(1,128)} %bitcast.13, s32[7,1,16]{2,1,0:T(1,128)} %bitcast.14, ...), custom_call_target="tpu_custom_call" | custom-call | tf_op jit(solution)/shard_map/pallas_call | solution.py:487
  62.1 2.0 %shard_map.65 = f32[12,4,12288]{2,1,0:T(4,128)} custom-call(s32[7,1,16]{2,1,0:T(1,128)S(1)} %get-tuple-element.8.table_ref, f32[6,3,48,256]{3,2,1,0:T(8,128)S(1)} %get-tuple-element.9.late_ref, f32[12,4,12288]{2,1,0:T(4,128)S(1)} %get-tuple-element.10.total_ref), custom_call_target="tpu_custom_call" | custom-call | tf_op jit(solution)/shard_map/pallas_call | solution.py:535

commit v7 on v6

--- a/solution.py
+++ b/solution.py
@@ -9,6 +9,7 @@
 
 MESH = pl.DeviceIdType.MESH
 AB_DEV = 48
+PARTS = 4
 CHUNK = 3
 PIECE = 8
 COLUMN = 16
@@ -111,6 +112,24 @@
             device_id_type=MESH,
         )
 
+    barrier = pltpu.get_barrier_semaphore()
+    for step in range(1, reach + 1):
+        pl.semaphore_signal(barrier, inc=1, device_id=target(-step), device_id_type=MESH)
+
+    @pl.when(is_source)
+    def _():
+        for helper in range(helpers):
+            pl.semaphore_signal(
+                barrier, inc=1, device_id=target(-COLUMN * (helpers - helper)), device_id_type=MESH
+            )
+
+    @pl.when(is_receiver)
+    def _():
+        for helper in range(helpers):
+            pl.semaphore_signal(
+                barrier, inc=1, device_id=target(-relay_off - COLUMN * (helpers - helper)), device_id_type=MESH
+            )
+
     col_copy = pltpu.make_async_copy(col_hbm, col_ref, in_sem.at[pieces + 1])
     count_copy = pltpu.make_async_copy(count_hbm, count_ref, in_sem.at[pieces + 2])
     frac_copy = pltpu.make_async_copy(frac_hbm, frac_ref, in_sem.at[pieces])
@@ -123,24 +142,6 @@
     for piece in range(pieces):
         flux_copy(piece).start()
     rows_copy.start()
-
-    barrier = pltpu.get_barrier_semaphore()
-    for step in range(1, reach + 1):
-        pl.semaphore_signal(barrier, inc=1, device_id=target(-step), device_id_type=MESH)
-
-    @pl.when(is_source)
-    def _():
-        for helper in range(helpers):
-            pl.semaphore_signal(
-                barrier, inc=1, device_id=target(-COLUMN * (helpers - helper)), device_id_type=MESH
-            )
-
-    @pl.when(is_receiver)
-    def _():
-        for helper in range(helpers):
-            pl.semaphore_signal(
-                barrier, inc=1, device_id=target(-relay_off - COLUMN * (helpers - helper)), device_id_type=MESH
-            )
 
     def merge_piece(block, piece, frac, total):
         parts = []
@@ -397,7 +398,7 @@
         late_copy(turn).wait()
 
 
-def settle_kernel(table_ref, late_ref, total_ref, out_hbm, out_ref, touched_ref, out_sem):
+def settle_kernel(table_hbm, late_ref, total_ref, out_hbm, out_ref, touched_ref, table_ref, out_sem, table_sem, block_sem):
     others, steps, _, block_rows = late_ref.shape
     num_kind, num_step, cells_dev = out_ref.shape
     atm_blocks = cells_dev // block_rows
@@ -407,9 +408,13 @@
     def cells_of(block):
         return pl.ds(pl.multiple_of(block * block_rows, block_rows), block_rows)
 
-    def emit(ref, block):
-        cells = cells_of(block)
-        return pltpu.make_async_copy(ref.at[:, :, cells], out_hbm.at[:, :, cells], out_sem)
+    table_copy = pltpu.make_async_copy(table_hbm, table_ref, table_sem)
+    table_copy.start()
+    whole = pltpu.make_async_copy(total_ref, out_hbm, out_sem)
+    for first in range(0, num_kind, num_kind // PARTS):
+        kinds = pl.ds(first, num_kind // PARTS)
+        pltpu.make_async_copy(total_ref.at[kinds], out_hbm.at[kinds], out_sem).start()
+    table_copy.wait()
 
     arrivals = []
     for turn in range(others):
@@ -420,28 +425,11 @@
     for turn, step, offset in arrivals:
         live = live + jnp.where(table_ref[offset, 0, first_slot + step] >= 0, 1, 0)
 
-    @pl.when(live == 0)
-    def _():
-        pltpu.make_async_copy(total_ref, out_hbm, out_sem).start()
-
     @pl.when(live > 0)
     def _():
         @pl.loop(0, atm_blocks, unroll=8)
         def _(block):
             touched_ref[block] = 0
-
-        for turn, step, offset in arrivals:
-            row = table_ref[offset, 0, first_slot + step]
-
-            @pl.when(row >= 0)
-            def _():
-                touched_ref[jnp.maximum(row, 0)] = 1
-
-        @pl.loop(0, atm_blocks)
-        def _(block):
-            @pl.when(touched_ref[block] == 0)
-            def _():
-                emit(total_ref, block).start()
 
         for turn, step, offset in arrivals:
             row = table_ref[offset, 0, first_slot + step]
@@ -450,8 +438,8 @@
             def _():
                 block = jnp.maximum(row, 0)
                 cells = cells_of(block)
-                fresh = touched_ref[block] == 1
-                touched_ref[block] = 2
+                fresh = touched_ref[block] == 0
+                touched_ref[block] = 1
 
                 @pl.when(fresh)
                 def _():
@@ -467,13 +455,25 @@
                             out_ref[kind, :, cells] + late_ref[turn, step, pl.ds(kind * num_step, num_step), :]
                         )
 
+    whole.wait()
+
+    @pl.when(live > 0)
+    def _():
+        def rewrite(block):
+            cells = cells_of(block)
+            return pltpu.make_async_copy(out_ref.at[:, :, cells], out_hbm.at[:, :, cells], block_sem.at[block])
+
         @pl.loop(0, atm_blocks)
         def _(block):
-            @pl.when(touched_ref[block] == 2)
+            @pl.when(touched_ref[block] == 1)
             def _():
-                emit(out_ref, block).start()
-
-    pltpu.make_async_copy(total_ref, out_hbm, out_sem).wait()
+                rewrite(block).start()
+
+        @pl.loop(0, atm_blocks)
+        def _(block):
+            @pl.when(touched_ref[block] == 1)
+            def _():
+                rewrite(block).wait()
 
 
 def on_device(sizes, tile_flux, tile_frac, weights, block_row, block_col, send_counts):
@@ -535,12 +535,15 @@
     settled = pl.pallas_call(
         settle_kernel,
         out_shape=jax.ShapeDtypeStruct((num_kind, num_step, AB_DEV * block_rows), jnp.float32),
-        in_specs=[pl.BlockSpec(memory_space=pltpu.SMEM)] + [pl.BlockSpec(memory_space=pltpu.VMEM)] * 2,
+        in_specs=[pl.BlockSpec(memory_space=pl.ANY)] + [pl.BlockSpec(memory_space=pltpu.VMEM)] * 2,
         out_specs=pl.BlockSpec(memory_space=pltpu.HBM),
         scratch_shapes=[
             pltpu.VMEM((num_kind, num_step, AB_DEV * block_rows), jnp.float32),
             pltpu.SMEM((AB_DEV,), jnp.int32),
+            pltpu.SMEM((num_off, 1, slots), jnp.int32),
             pltpu.SemaphoreType.DMA,
+            pltpu.SemaphoreType.DMA,
+            pltpu.SemaphoreType.DMA((AB_DEV,)),
         ],
         compiler_params=pltpu.CompilerParams(vmem_limit_bytes=12 * 1024 * 1024),
     )(tables, late, total)

time: 64.5 us -> 64.3 us (level)
  no operation moved by 1% of the time
where the time goes in v7:
time: 64.3 us; the launch traced here: 63.9 us
  Pallas kernels  63.9 us (99%)
    pallas_call x1, Pallas kernels, on_device(): pl.pallas_call(functools.partial(send_kernel, sizes), out_shape=(jax.Shap...  62 us
    pallas_call x1, Pallas kernels, on_device(): pl.pallas_call(settle_kernel, out_shape=jax.ShapeDtypeStruct((num_kind, n...  1.85 us

profile of v7, /device:TPU:1, one launch (start us, length us, event | category | flops | bytes accessed | tf_op | source)
XLA Modules:
  0.0 63.9 jit_solution(4999844989459711230)
XLA Ops:
  0.0 62.0 %shard_map.64 = (f32[6,3,48,256]{3,2,1,0:T(8,128)S(1)}, f32[12,4,12288]{2,1,0:T(4,128)S(1)}, s32[7,1,16]{2,1,0:T(1,128)S(1)}) custom-call(bf16[4,12,32,8,128]{4,3,2,1,0:T(8,128)(2,1)} %bitcast.11, f32[32,8,128]{2,1,0:T(8,128)} %bitcast.12, bf16[7,16,256,128]{3,2,1,0:T(8,128)(2,1)} %bitcast.10, s32[7,1,16]{2,1,0:T(1,128)} %bitcast.13, s32[7,1,16]{2,1,0:T(1,128)} %bitcast.14, ...), custom_call_target="tpu_custom_call" | custom-call | tf_op jit(solution)/shard_map/pallas_call | solution.py:487
  62.0 1.8 %shard_map.65 = f32[12,4,12288]{2,1,0:T(4,128)} custom-call(s32[7,1,16]{2,1,0:T(1,128)S(1)} %get-tuple-element.8.table_hbm, f32[6,3,48,256]{3,2,1,0:T(8,128)S(1)} %get-tuple-element.9.late_ref, f32[12,4,12288]{2,1,0:T(4,128)S(1)} %get-tuple-element.10.total_ref), custom_call_target="tpu_custom_call" | custom-call | tf_op jit(solution)/shard_map/pallas_call | solution.py:535

commit v8 on v7

--- a/solution.py
+++ b/solution.py
@@ -70,6 +70,12 @@
     def offset_of(turn):
         return (reach - turn // 2) * (1 - 2 * (turn % 2))
 
+    swap = jnp.where(is_helper, 2, 0)
+
+    def order(i):
+        pair = i % others // 2
+        return i + swap * (pair % 2 - pair // 2)
+
     def plan(i):
         return i // others, offset_of(i % others)
 
@@ -266,7 +272,7 @@
 
     @pl.loop(0, sends)
     def _(i):
-        chunk, off = plan(i)
+        chunk, off = plan(order(i))
 
         @pl.when(i < others)
         def _():
@@ -278,7 +284,7 @@
 
         @pl.when(jnp.logical_and(jnp.logical_and(i > 0, i <= early), jnp.logical_not(relayed)))
         def _():
-            chunk_copy(i - 1).start()
+            chunk_copy(order(i - 1)).start()
 
         @pl.when(relayed)
         def _():
@@ -293,13 +299,13 @@
 
         @pl.when(i > early)
         def _():
-            late_copy(i - 1 - early).start()
+            late_copy(order(i - 1) - early).start()
 
     own_table = pltpu.make_async_copy(live_rows_ref.at[reach], tables_hbm.at[reach], in_sem.at[0])
     own_table.start()
     weight_copy(first_part(reach), first_weight.at[reach]).wait()
     multiply(merged_ref[col_ref[reach, 0, 0]], reach, 0)
-    late_copy(others - 1).start()
+    late_copy(order(sends - 1) - early).start()
 
     rest_copy(reach).wait()
 

time: 64.3 us -> 65.1 us (1.012); the launches traced: 63.9 us -> 63.9 us
  no operation moved by 1% of the time
where the time goes in v8:
time: 65.1 us; the launch traced here: 63.9 us
  Pallas kernels  63.9 us (98%)
    pallas_call x1, Pallas kernels, on_device(): pl.pallas_call(functools.partial(send_kernel, sizes), out_shape=(jax.Shap...  62 us
    pallas_call x1, Pallas kernels, on_device(): pl.pallas_call(settle_kernel, out_shape=jax.ShapeDtypeStruct((num_kind, n...  1.85 us

profile of v8, /device:TPU:1, one launch (start us, length us, event | category | flops | bytes accessed | tf_op | source)
XLA Modules:
  0.0 63.9 jit_solution(1874391840611264975)
XLA Ops:
  0.0 62.0 %shard_map.64 = (f32[6,3,48,256]{3,2,1,0:T(8,128)S(1)}, f32[12,4,12288]{2,1,0:T(4,128)S(1)}, s32[7,1,16]{2,1,0:T(1,128)S(1)}) custom-call(bf16[4,12,32,8,128]{4,3,2,1,0:T(8,128)(2,1)} %bitcast.11, f32[32,8,128]{2,1,0:T(8,128)} %bitcast.12, bf16[7,16,256,128]{3,2,1,0:T(8,128)(2,1)} %bitcast.10, s32[7,1,16]{2,1,0:T(1,128)} %bitcast.13, s32[7,1,16]{2,1,0:T(1,128)} %bitcast.14, ...), custom_call_target="tpu_custom_call" | custom-call | tf_op jit(solution)/shard_map/pallas_call | solution.py:493
  62.0 1.8 %shard_map.65 = f32[12,4,12288]{2,1,0:T(4,128)} custom-call(s32[7,1,16]{2,1,0:T(1,128)S(1)} %get-tuple-element.8.table_hbm, f32[6,3,48,256]{3,2,1,0:T(8,128)S(1)} %get-tuple-element.9.late_ref, f32[12,4,12288]{2,1,0:T(4,128)S(1)} %get-tuple-element.10.total_ref), custom_call_target="tpu_custom_call" | custom-call | tf_op jit(solution)/shard_map/pallas_call | solution.py:541
